TPU v7x, 32 devices: a whole 2x2x4 slice. The times are simulated.
32 devices in a mesh: fsdp: 16 (over z, y, x), sub: 2 (over core).
Axes of the slice: x: 2, y: 2, z: 4, core: 2. Of those that a mesh axis runs over, the one named last changes fastest.
Arguments:
- inputs: bfloat16 [64, 512, 768], P(('fsdp', 'sub')), may hold values from -6 to 6
- lengths: int32 [64], P(('fsdp', 'sub')), may hold values from 257 to 512, as said below
- positions: int32 [64, 128], P(('fsdp', 'sub')), may hold values from 0 to 512, as said below
- masked_output_gradient: bfloat16 [64, 128, 768], P(('fsdp', 'sub')), may hold values from -6 to 6
- w_query: bfloat16 [768, 768], P(('fsdp', 'sub')), may hold values from -0.21875 to 0.21875
- b_query: bfloat16 [768], P(('fsdp', 'sub')), may hold values from -3 to 3
- w_key: bfloat16 [768, 768], P(('fsdp', 'sub')), may hold values from -0.21875 to 0.21875
- w_value: bfloat16 [768, 768], P(('fsdp', 'sub')), may hold values from -0.21875 to 0.21875
- b_value: bfloat16 [768], P(('fsdp', 'sub')), may hold values from -3 to 3
- w_out: bfloat16 [768, 768], P(('fsdp', 'sub')), may hold values from -1.75 to 1.75
- b_out: bfloat16 [768], P(('fsdp', 'sub')), may hold values from -3 to 3
- gain_attn: bfloat16 [768], P(('fsdp', 'sub')), may hold values from 0.5 to 1.5
- shift_attn: bfloat16 [768], P(('fsdp', 'sub')), may hold values from -3 to 3
- w_up: bfloat16 [768, 3072], P(('fsdp', 'sub')), may hold values from -0.21875 to 0.21875
- b_up: bfloat16 [3072], P(('fsdp', 'sub')), may hold values from -3 to 3
- w_down: bfloat16 [3072, 768], P(('fsdp', 'sub')), may hold values from -0.109375 to 0.109375
- b_down: bfloat16 [768], P(('fsdp', 'sub')), may hold values from -3 to 3
- gain_ffn: bfloat16 [768], P(('fsdp', 'sub')), may hold values from 0.5 to 1.5
- shift_ffn: bfloat16 [768], P(('fsdp', 'sub')), may hold values from -3 to 3
Outputs:
- output: bfloat16 [64, 512, 768], P(('fsdp', 'sub'))
- grad_inputs: bfloat16 [64, 512, 768], P(('fsdp', 'sub'))
- grad_w_query: float32 [768, 768], P(('fsdp', 'sub'))
- grad_b_query: float32 [768], P(('fsdp', 'sub'))
- grad_w_key: float32 [768, 768], P(('fsdp', 'sub'))
- grad_w_value: float32 [768, 768], P(('fsdp', 'sub'))
- grad_b_value: float32 [768], P(('fsdp', 'sub'))
- grad_w_out: float32 [768, 768], P(('fsdp', 'sub'))
- grad_b_out: float32 [768], P(('fsdp', 'sub'))
- grad_gain_attn: float32 [768], P(('fsdp', 'sub'))
- grad_shift_attn: float32 [768], P(('fsdp', 'sub'))
- grad_w_up: float32 [768, 3072], P(('fsdp', 'sub'))
- grad_b_up: float32 [3072], P(('fsdp', 'sub'))
- grad_w_down: float32 [3072, 768], P(('fsdp', 'sub'))
- grad_b_down: float32 [768], P(('fsdp', 'sub'))
- grad_gain_ffn: float32 [768], P(('fsdp', 'sub'))
- feedforward_shift_gradient: float32 [768], P(('fsdp', 'sub'))
Inputs may be any that keep to these rules, and one draw needn't show every extreme that they name: `lengths`: the valid tokens of a sequence come first; the first sequence is full. In each sequence the used slots come first, from 16 to 128 of them, holding distinct positions below the sequence's length; the other slots hold 512. Some sequence uses all 128 slots.
All inputs are finite; a program needn't handle non-finite values.
Results may differ from a plain program's by a relative error of at most 0.014.
The roundings to bfloat16 on the way count: a program that leaves them out, or rounds other values in their place, can miss the bound.
Values may be sent and summed in bfloat16 or wider, within the bound.
A program may use at most 192 MiB of HBM per device.

v0:
```python
import jax
import jax.numpy as jnp
from jax import lax
from jax.sharding import PartitionSpec as P

HD = 64


EPSILON = 1e-06


def layer_norm(values, gain, shift):
    average = jnp.mean(values, axis=-1, keepdims=True)
    centered = values - average
    variance = jnp.mean(centered * centered, axis=-1, keepdims=True)
    return centered * lax.rsqrt(variance + EPSILON) * gain + shift


def gelu_exact(values):
    return jax.nn.gelu(values, approximate=False)


def project(rows_low, weight):
    return jnp.dot(rows_low, weight, preferred_element_type=jnp.float32)


def reverse_projection(grad_low, weight):
    return lax.dot_general(
        grad_low, weight, (((1,), (1,)), ((), ())), preferred_element_type=jnp.float32
    )


def weight_grad(rows_low, grad_low):
    return lax.dot_general(
        rows_low, grad_low, (((0,), (0,)), ((), ())), preferred_element_type=jnp.float32
    )


def column_sum(grad_low):
    return jnp.sum(grad_low.astype(jnp.float32), axis=0)


def attention_scores(query_heads, key_heads, valid_keys, scale):
    scores = (
        jnp.einsum("sqhd,skhd->shqk", query_heads, key_heads, preferred_element_type=jnp.float32)
        * scale
    )
    return jnp.where(valid_keys[:, None, None, :], scores, -1e30)


def body(
    inputs,
    lengths,
    positions,
    masked_output_gradient,
    w_query,
    b_query,
    w_key,
    w_value,
    b_value,
    w_out,
    b_out,
    gain_attn,
    shift_attn,
    w_up,
    b_up,
    w_down,
    b_down,
    gain_ffn,
    shift_ffn,
):
    seq_count, seq_slots, width = inputs.shape
    head_count = width // HD
    scale = HD ** (-0.5)
    row_count = seq_count * seq_slots
    head_shape = (seq_count, seq_slots, head_count, HD)
    token_ids = jnp.arange(seq_slots, dtype=jnp.int32)
    valid_keys = token_ids[None, :] < lengths[:, None]
    (
        query_weight,
        key_weight,
        value_weight,
        out_weight,
        query_bias,
        value_bias,
        out_bias,
        norm1_gain,
        norm1_shift,
    ) = (
        lax.all_gather(w_query, ("fsdp", "sub"), axis=0, tiled=True),
        lax.all_gather(w_key, ("fsdp", "sub"), axis=0, tiled=True),
        lax.all_gather(w_value, ("fsdp", "sub"), axis=0, tiled=True),
        lax.all_gather(w_out, ("fsdp", "sub"), axis=0, tiled=True),
        lax.all_gather(b_query, ("fsdp", "sub"), axis=0, tiled=True),
        lax.all_gather(b_value, ("fsdp", "sub"), axis=0, tiled=True),
        lax.all_gather(b_out, ("fsdp", "sub"), axis=0, tiled=True),
        lax.all_gather(gain_attn, ("fsdp", "sub"), axis=0, tiled=True),
        lax.all_gather(shift_attn, ("fsdp", "sub"), axis=0, tiled=True),
    )
    flat_in = inputs.reshape(row_count, width)
    input_rows = flat_in.astype(jnp.float32)
    query_low = (project(flat_in, query_weight) + query_bias.astype(jnp.float32)).astype(
        jnp.bfloat16
    )
    keys_low = project(flat_in, key_weight).astype(jnp.bfloat16)
    values_low = (project(flat_in, value_weight) + value_bias.astype(jnp.float32)).astype(
        jnp.bfloat16
    )
    query_heads = query_low.reshape(head_shape)
    key_heads = keys_low.reshape(head_shape)
    value_heads = values_low.reshape(head_shape)
    scores = attention_scores(query_heads, key_heads, valid_keys, scale)
    row_top = jnp.max(scores, axis=-1, keepdims=True)
    expon = jnp.exp(scores - row_top)
    row_total = jnp.sum(expon, axis=-1, keepdims=True)
    log_total = row_top + jnp.log(row_total)
    probs_low = (expon / row_total).astype(jnp.bfloat16)
    attention_mixed = jnp.einsum(
        "shqk,skhd->sqhd", probs_low, value_heads, preferred_element_type=jnp.float32
    )
    attended_low = attention_mixed.reshape(row_count, width).astype(jnp.bfloat16)
    branch = project(attended_low, out_weight) + out_bias.astype(jnp.float32)
    middle, norm1_pull = jax.vjp(
        layer_norm,
        input_rows + branch,
        norm1_gain.astype(jnp.float32),
        norm1_shift.astype(jnp.float32),
    )
    middle_low = middle.astype(jnp.bfloat16)
    up_weight, up_bias, down_weight, downward_bias, norm2_gain, norm2_shift = (
        lax.all_gather(w_up, ("fsdp", "sub"), axis=0, tiled=True),
        lax.all_gather(b_up, ("fsdp", "sub"), axis=0, tiled=True),
        lax.all_gather(w_down, ("fsdp", "sub"), axis=0, tiled=True),
        lax.all_gather(b_down, ("fsdp", "sub"), axis=0, tiled=True),
        lax.all_gather(gain_ffn, ("fsdp", "sub"), axis=0, tiled=True),
        lax.all_gather(shift_ffn, ("fsdp", "sub"), axis=0, tiled=True),
    )
    hidden = project(middle_low, up_weight) + up_bias.astype(jnp.float32)
    active, gelu_pull = jax.vjp(gelu_exact, hidden)
    active_low = active.astype(jnp.bfloat16)
    second_branch = project(active_low, down_weight) + downward_bias.astype(jnp.float32)
    output, norm2_pull = jax.vjp(
        layer_norm,
        middle + second_branch,
        norm2_gain.astype(jnp.float32),
        norm2_shift.astype(jnp.float32),
    )
    position_matches = (positions[:, :, None] == token_ids[None, None, :]).astype(jnp.bfloat16)
    cotangent = jnp.einsum(
        "efw,efv->ewv", position_matches, masked_output_gradient, preferred_element_type=jnp.float32
    ).reshape(row_count, width)
    grad_sum2, grad_gain2, grad_shift2 = norm2_pull(cotangent)
    up_back, down_back = (
        lax.all_gather(w_up, ("fsdp", "sub"), axis=0, tiled=True),
        lax.all_gather(w_down, ("fsdp", "sub"), axis=0, tiled=True),
    )
    second_grad = grad_sum2.astype(jnp.bfloat16)
    grad_down = weight_grad(active_low, second_grad)
    grad_down_bias = column_sum(second_grad)
    (grad_hidden,) = gelu_pull(reverse_projection(second_grad, down_back))
    hidden_grad = grad_hidden.astype(jnp.bfloat16)
    grad_up = weight_grad(middle_low, hidden_grad)
    grad_up_bias = column_sum(hidden_grad)
    grad_middle = grad_sum2 + reverse_projection(hidden_grad, up_back)
    ffn_result = (
        lax.psum_scatter(grad_up, ("fsdp", "sub"), scatter_dimension=0, tiled=True),
        lax.psum_scatter(grad_up_bias, ("fsdp", "sub"), scatter_dimension=0, tiled=True),
        lax.psum_scatter(grad_down, ("fsdp", "sub"), scatter_dimension=0, tiled=True),
        lax.psum_scatter(grad_down_bias, ("fsdp", "sub"), scatter_dimension=0, tiled=True),
        lax.psum_scatter(grad_gain2, ("fsdp", "sub"), scatter_dimension=0, tiled=True),
        lax.psum_scatter(grad_shift2, ("fsdp", "sub"), scatter_dimension=0, tiled=True),
    )
    grad_residual, grad_gain1, grad_shift1 = norm1_pull(grad_middle)
    branch_grad = grad_residual.astype(jnp.bfloat16)
    grad_out = weight_grad(attended_low, branch_grad)
    grad_out_bias = column_sum(branch_grad)
    query_back, key_back, value_back, out_back = (
        lax.all_gather(w_query, ("fsdp", "sub"), axis=0, tiled=True),
        lax.all_gather(w_key, ("fsdp", "sub"), axis=0, tiled=True),
        lax.all_gather(w_value, ("fsdp", "sub"), axis=0, tiled=True),
        lax.all_gather(w_out, ("fsdp", "sub"), axis=0, tiled=True),
    )
    attended_grad = (
        reverse_projection(branch_grad, out_back).astype(jnp.bfloat16).reshape(head_shape)
    )
    scores_again = attention_scores(query_heads, key_heads, valid_keys, scale)
    probs = jnp.exp(scores_again - log_total)
    probs_again = probs.astype(jnp.bfloat16)
    probs_grad = jnp.einsum(
        "sqhd,skhd->shqk", attended_grad, value_heads, preferred_element_type=jnp.float32
    )
    values_grad = jnp.einsum(
        "shqk,sqhd->skhd", probs_again, attended_grad, preferred_element_type=jnp.float32
    )
    values_grad = values_grad.astype(jnp.bfloat16).reshape(row_count, width)
    inner_sum = jnp.sum(probs * probs_grad, axis=-1, keepdims=True)
    scores_grad = (probs * (probs_grad - inner_sum)).astype(jnp.bfloat16)
    query_grad = jnp.einsum(
        "shqk,skhd->sqhd", scores_grad, key_heads, preferred_element_type=jnp.float32
    )
    query_grad = (query_grad * scale).astype(jnp.bfloat16).reshape(row_count, width)
    keys_grad = jnp.einsum(
        "shqk,sqhd->skhd", scores_grad, query_heads, preferred_element_type=jnp.float32
    )
    keys_grad = (keys_grad * scale).astype(jnp.bfloat16).reshape(row_count, width)
    grad_query = weight_grad(flat_in, query_grad)
    grad_query_bias = column_sum(query_grad)
    grad_key = weight_grad(flat_in, keys_grad)
    grad_value = weight_grad(flat_in, values_grad)
    value_bias_gradient = column_sum(values_grad)
    grad_input = (
        grad_residual
        + reverse_projection(query_grad, query_back)
        + reverse_projection(keys_grad, key_back)
        + reverse_projection(values_grad, value_back)
    )
    attn_result = (
        lax.psum_scatter(grad_query, ("fsdp", "sub"), scatter_dimension=0, tiled=True),
        lax.psum_scatter(grad_query_bias, ("fsdp", "sub"), scatter_dimension=0, tiled=True),
        lax.psum_scatter(grad_key, ("fsdp", "sub"), scatter_dimension=0, tiled=True),
        lax.psum_scatter(grad_value, ("fsdp", "sub"), scatter_dimension=0, tiled=True),
        lax.psum_scatter(value_bias_gradient, ("fsdp", "sub"), scatter_dimension=0, tiled=True),
        lax.psum_scatter(grad_out, ("fsdp", "sub"), scatter_dimension=0, tiled=True),
        lax.psum_scatter(grad_out_bias, ("fsdp", "sub"), scatter_dimension=0, tiled=True),
        lax.psum_scatter(grad_gain1, ("fsdp", "sub"), scatter_dimension=0, tiled=True),
        lax.psum_scatter(grad_shift1, ("fsdp", "sub"), scatter_dimension=0, tiled=True),
    )
    return (
        output.astype(jnp.bfloat16).reshape(inputs.shape),
        grad_input.astype(jnp.bfloat16).reshape(inputs.shape),
        attn_result[0],
        attn_result[1],
        attn_result[2],
        attn_result[3],
        attn_result[4],
        attn_result[5],
        attn_result[6],
        attn_result[7],
        attn_result[8],
        ffn_result[0],
        ffn_result[1],
        ffn_result[2],
        ffn_result[3],
        ffn_result[4],
        ffn_result[5],
    )


def solution(mesh):
    return jax.shard_map(
        body,
        mesh=mesh,
        in_specs=(
            P(("fsdp", "sub"), None, None),
            P(("fsdp", "sub")),
            P(("fsdp", "sub"), None),
            P(("fsdp", "sub"), None, None),
            P(("fsdp", "sub"), None),
            P(("fsdp", "sub")),
            P(("fsdp", "sub"), None),
            P(("fsdp", "sub"), None),
            P(("fsdp", "sub")),
            P(("fsdp", "sub"), None),
            P(("fsdp", "sub")),
            P(("fsdp", "sub")),
            P(("fsdp", "sub")),
            P(("fsdp", "sub"), None),
            P(("fsdp", "sub")),
            P(("fsdp", "sub"), None),
            P(("fsdp", "sub")),
            P(("fsdp", "sub")),
            P(("fsdp", "sub")),
        ),
        out_specs=(
            P(("fsdp", "sub"), None, None),
            P(("fsdp", "sub"), None, None),
            P(("fsdp", "sub"), None),
            P(("fsdp", "sub")),
            P(("fsdp", "sub"), None),
            P(("fsdp", "sub"), None),
            P(("fsdp", "sub")),
            P(("fsdp", "sub"), None),
            P(("fsdp", "sub")),
            P(("fsdp", "sub")),
            P(("fsdp", "sub")),
            P(("fsdp", "sub"), None),
            P(("fsdp", "sub")),
            P(("fsdp", "sub"), None),
            P(("fsdp", "sub")),
            P(("fsdp", "sub")),
            P(("fsdp", "sub")),
        ),
        check_vma=False,
    )
```

profile of v0, /device:TPU:0, one launch (start us, length us, event | category | flops | bytes accessed | tf_op | source)
XLA Modules:
  0.0 1130.4 jit_solution(4144503927960513225)
XLA Ops:
  19.5 42.6 %all-reduce.19 = (bf16[768]{0:T(1024)(128)(2,1)S(1)}, bf16[768]{0:T(1024)(128)(2,1)S(1)}, bf16[768]{0:T(1024)(128)(2,1)S(1)}, bf16[768]{0:T(1024)(128)(2,1)S(1)}...) all-reduce(bf16[768]{0:T(1024)(128)(2,1)S(1)} %dynamic-update-slice, ...), channel_id=1, replica_groups=mesh['fsdp'=16,'sub'=2] {'fsdp','sub'}, use_global_device_ids=true, to_apply=%add.1 | all-reduce | flops 9216 | bytes 36864
  65.1 3.5 fusion.52
  68.6 3.1 add_convert_fusion.4
  72.5 2.4 reshape.170
  74.9 48.7 %all-gather.9.cloned.1.call-done = bf16[768,768]{1,0:T(8,128)(2,1)} async-done(((bf16[24,768]{1,0:T(8,128)(2,1)}), bf16[768,768]{1,0:T(8,128)(2,1)}) %all-gather.9.cloned.1.call-update) | async-done | bytes 1179664 | tf_op jit(solution)/shard_map/all_gather | solution.py:90
  123.6 3.1 add_convert_fusion.3
  127.5 1.2 reshape.171
  128.7 50.6 %all-gather.11.cloned.1.call-done = bf16[768,768]{1,0:T(8,128)(2,1)} async-done(((bf16[24,768]{1,0:T(8,128)(2,1)}), bf16[768,768]{1,0:T(8,128)(2,1)}) %all-gather.11.cloned.1.call-update) | async-done | bytes 1179664 | tf_op jit(solution)/shard_map/all_gather | solution.py:91
  179.3 3.1 convolution_convert_fusion.1
  182.5 1.6 copy.76
  184.1 2.9 reshape.172
  187.0 11.1 fusion.12
  198.1 11.2 fusion
  209.3 11.6 %fusion.24 = bf16[2,512,12,64]{1,3,2,0:T(8,128)(2,1)S(1)} fusion(f32[2,12,512]{2,1,0:T(8,128)S(1)} %fusion, f32[2,12,512]{2,1,0:T(8,128)S(1)} %get-tuple-element.102, f32[2,12,512,512]{2,3,1,0:T(8,128)} %get-tuple-element.103, pred[2,512]{1,0:T(4,128)(4,1)S(1)} %iota_compare_fusion.2, bf16[2,512,12,64]{1,0,3,2:T(2,128)(2,1)S(1)} %copy-done.11), kind=kOutput, calls=%fused_computation.67 | convolution fusion | flops 837550080 | bytes 28410880 | tf_op jit(solution)/shard_map/shqk,skhd->sqhd/dot_general | solution.py:118
  220.9 1.6 copy.81
  222.6 1.6 copy.107
  224.1 10.8 all-gather.13.cloned.1.call-done
  234.9 3.9 fusion.50
  240.0 60.2 %all-gather.15.cloned.1.call-done = bf16[768,3072]{1,0:T(8,128)(2,1)} async-done(((bf16[24,3072]{1,0:T(8,128)(2,1)}), bf16[768,3072]{1,0:T(8,128)(2,1)}) %all-gather.15.cloned.1.call-update) | async-done | bytes 4718608 | tf_op jit(solution)/shard_map/all_gather | solution.py:131
  300.2 35.8 %multiply_convert_fusion.1 = (bf16[1024,3072]{1,0:T(8,128)(2,1)}, f32[1024,3072]{1,0:T(8,128)}, f32[1024,3072]{1,0:T(8,128)}) fusion(f32[3072]{0:T(1024)S(1)} %copy-done.27, bf16[768,3072]{1,0:T(8,128)(2,1)} %all-gather.15.cloned.1.call-done, f32[1024,768]{1,0:T(8,128)S(1)} %get-tuple-element.105, f32[768]{0:T(1024)S(1)} %convert_element_type.129, ...), kind=kOutput, calls=%fused_computation.14 | convolution fusion | flops 5043388416 | bytes 39348224 | tf_op jit(solution)/shard_map/dot_general | solution.py:24
  336.0 28.9 %all-gather.17.cloned.1.call-done = bf16[3072,768]{1,0:T(8,128)(2,1)} async-done(((bf16[96,768]{1,0:T(8,128)(2,1)}), bf16[3072,768]{1,0:T(8,128)(2,1)}) %all-gather.17.cloned.1.call-update) | async-done | bytes 4718608 | tf_op jit(solution)/shard_map/all_gather | solution.py:133
  364.9 9.3 fusion.51
  374.8 1.3 copy-done.5
  376.1 1.6 fusion.13
  377.7 2.7 fusion.48
  380.5 1.5 convert_reduce_fusion.1
  382.0 18.3 %convert_reduce_fusion = (f32[3072]{0:T(1024)S(1)}, bf16[1024,3072]{1,0:T(8,128)(2,1)}) fusion(f32[1024,3072]{1,0:T(8,128)} %get-tuple-element.100, bf16[1024,768]{1,0:T(8,128)(2,1)} %get-tuple-element.92, bf16[3072,768]{1,0:T(8,128)(2,1)} %all-gather.17.cloned.1.call-done, f32[1024,3072]{1,0:T(8,128)} %get-tuple-element.106, f32[3072]{0:T(1024)S(1)} %copy-done.27), kind=kOutput, calls=%fused_computation.11 | convolution fusion | flops 4885312512 | bytes 37773312 | tf_op jit(solution)/shard_map/dot_general | solution.py:28
  400.3 9.5 multiply_reduce_fusion.1
  409.9 1.6 fusion.47
  411.5 1.6 copy-done.3
  413.5 1.2 copy-done.18
  414.6 2.8 fusion.55
  417.4 4.3 convolution_convert_fusion
  421.7 2.6 copy.82
  424.3 3.9 reshape.175
  428.3 11.9 %convert_reduce_fusion.3 = (f32[12,64]{1,0:T(8,128)S(1)}, bf16[2,512,12,64]{1,3,2,0:T(8,128)(2,1)S(1)}) fusion(f32[2,12,512]{2,1,0:T(8,128)S(1)} %copy-done.20, f32[2,12,512,512]{2,3,1,0:T(8,128)} %get-tuple-element.103, pred[2,512]{1,0:T(4,128)(4,1)S(1)} %copy-done.22, bf16[2,512,12,64]{1,0,3,2:T(2,128)(2,1)} %reshape.175), kind=kOutput, calls=%fused_computation.38 | convolution fusion | flops 832830720 | bytes 28364800 | tf_op jit(solution)/shard_map/shqk,sqhd->skhd/dot_general | solution.py:192
  440.2 1.6 copy.93
  442.3 1.2 copy-done.9
  443.4 2.9 convolution_bitcast_fusion
  446.3 3.1 copy.105
  449.3 20.0 %multiply_reduce_fusion = (f32[2,12,512]{2,1,0:T(8,128)S(1)}, f32[2,12,512,512]{2,3,1,0:T(8,128)}) fusion(f32[2,12,512]{2,1,0:T(8,128)S(1)} %copy-done.20, f32[2,12,512,512]{2,3,1,0:T(8,128)} %get-tuple-element.103, pred[2,512]{1,0:T(4,128)(4,1)S(1)} %copy-done.22, bf16[2,512,12,64]{1,0,3,2:T(2,128)(2,1)} %reshape.170, bf16[2,512,12,64]{1,0,3,2:T(2,128)(2,1)} %reshape.175), kind=kOutput, calls=%fused_computation.1 | convolution fusion | flops 836751360 | bytes 53576704 | tf_op jit(solution)/shard_map/sqhd,skhd->shqk/dot_general | solution.py:189
  469.4 18.2 %multiply_convert_fusion = bf16[2,12,512,512]{2,3,1,0:T(8,128)(2,1)S(1)} fusion(f32[2,12,512,512]{2,3,1,0:T(8,128)} %get-tuple-element.111, f32[2,12,512]{2,1,0:T(8,128)S(1)} %get-tuple-element.110, f32[2,12,512]{2,1,0:T(8,128)S(1)} %copy-done.20, f32[2,12,512,512]{2,3,1,0:T(8,128)} %get-tuple-element.103, pred[2,512]{1,0:T(4,128)(4,1)S(1)} %copy-done.22), kind=kLoop, calls=%fused_computation | loop fusion | flops 37748736 | bytes 63013888 | tf_op jit(solution)/shard_map/convert_element_type | solution.py:197
  487.6 2.2 convert_reduce_fusion.4
  489.8 2.3 copy-done.2
  492.1 1.6 copy.87
  494.2 1.1 copy-done.12
  495.3 2.8 convolution_bitcast_fusion.2
  498.1 3.1 copy.101
  501.3 9.1 fusion.23
  510.3 1.6 copy.90
  513.5 2.8 convolution_bitcast_fusion.1
  516.4 3.3 copy.103
  519.7 10.7 fusion.43
  530.4 1.3 copy-done.17
  531.8 10.2 fusion.56
  542.6 39.9 %all-reduce.18 = (f32[768]{0:T(1024)S(1)}, f32[768]{0:T(1024)S(1)}, f32[768]{0:T(1024)S(1)}, f32[768]{0:T(1024)S(1)}, f32[768]{0:T(1024)S(1)}, /*index=5*/f32[30...) all-reduce(f32[768]{0:T(1024)S(1)} %reduce_sum.218, ...), channel_id=3, replica_groups=mesh['fsdp'=16,'sub'=2] {'fsdp','sub'}, use_global_device_ids=true, to_apply=%region_13.14.clone | all-reduce | flops 9216 | bytes 73728
  587.8 1.5 fusion.53
  589.6 1.4 fusion.54
  592.3 3.2 add_convert_fusion.1
  595.5 35.5 %reduce-scatter.23.cloned.1.call-done = f32[24,768]{1,0:T(8,128)} async-done(((f32[768,768]{1,0:T(8,128)}), f32[24,768]{1,0:T(8,128)}) %reduce-scatter.23.cloned.1.call-update) | async-done | bytes 73744
  631.0 104.5 %reduce-scatter.19.cloned.1.call-done = f32[24,768]{1,0:T(8,128)} async-done(((f32[768,768]{1,0:T(8,128)}), f32[24,768]{1,0:T(8,128)}) %reduce-scatter.19.cloned.1.call-update) | async-done | bytes 73744
  735.5 104.4 %reduce-scatter.21.cloned.1.call-done = f32[24,768]{1,0:T(8,128)} async-done(((f32[768,768]{1,0:T(8,128)}), f32[24,768]{1,0:T(8,128)}) %reduce-scatter.21.cloned.1.call-update) | async-done | bytes 73744
  839.9 142.0 %reduce-scatter.15.cloned.1.call-done = f32[24,3072]{1,0:T(8,128)} async-done(((f32[768,3072]{1,0:T(8,128)}), f32[24,3072]{1,0:T(8,128)}) %reduce-scatter.15.cloned.1.call-update) | async-done | bytes 294928 | tf_op jit(solution)/shard_map/reduce_scatter | solution.py:166
  981.9 141.5 %reduce-scatter.17.cloned.1.call-done = f32[96,768]{1,0:T(8,128)} async-done(((f32[3072,768]{1,0:T(8,128)}), f32[96,768]{1,0:T(8,128)}) %reduce-scatter.17.cloned.1.call-update) | async-done | bytes 294928 | tf_op jit(solution)/shard_map/reduce_scatter | solution.py:168
  (145 shorter events, 29.0 us)
Async XLA Ops:
  7.2 57.9 %copy-start = (bf16[2,128,768]{2,1,0:T(8,128)(2,1)S(1)}, bf16[2,128,768]{2,1,0:T(8,128)(2,1)}, u32[]{:S(2)}) copy-start(bf16[2,128,768]{2,1,0:T(8,128)(2,1)} %param.22) | copy-start | bytes 1179652
  7.2 61.4 %all-gather.7.cloned.1.call-start = ((), (), s32[]{:S(2)}) async-start(), calls=%async_computation.6 | async-start | bytes 1216512 | tf_op jit(solution)/shard_map/all_gather | solution.py:92
  7.9 115.6 %all-gather.9.cloned.1.call-start = ((), (), s32[]{:S(2)}) async-start(), calls=%async_computation.7 | async-start | bytes 1216512 | tf_op jit(solution)/shard_map/all_gather | solution.py:90
  8.7 170.6 %all-gather.11.cloned.1.call-start = ((), (), s32[]{:S(2)}) async-start(), calls=%async_computation.8 | async-start | bytes 1216512 | tf_op jit(solution)/shard_map/all_gather | solution.py:91
  9.4 225.5 %all-gather.13.cloned.1.call-start = ((), (), s32[]{:S(2)}) async-start(), calls=%async_computation.9 | async-start | bytes 1216512 | tf_op jit(solution)/shard_map/all_gather | solution.py:93
  10.0 290.2 %all-gather.15.cloned.1.call-start = ((), (), s32[]{:S(2)}) async-start(), calls=%async_computation.10 | async-start | bytes 4866048 | tf_op jit(solution)/shard_map/all_gather | solution.py:131
  10.6 354.3 %all-gather.17.cloned.1.call-start = ((), (), s32[]{:S(2)}) async-start(), calls=%async_computation.11 | async-start | bytes 4866048 | tf_op jit(solution)/shard_map/all_gather | solution.py:133
  11.2 584.4 %reduce-scatter.13.cloned.1.call-start = ((), (), s32[]{:S(2)}) async-start(), calls=%async_computation.12 | async-start | bytes 2433024 | tf_op jit(solution)/shard_map/reduce_scatter | solution.py:223
  11.9 197.3 %copy-start.21 = (pred[2,512]{1,0:T(4,128)(4,1)}, pred[2,512]{1,0:T(4,128)(4,1)S(1)}, u32[]{:S(2)}) copy-start(pred[2,512]{1,0:T(4,128)(4,1)S(1)} %iota_compare_fusion.2) | copy-start | bytes 3076
  71.7 51.8 %copy-start.29 = (f32[768]{0:T(1024)S(1)}, f32[768]{0:T(1024)}, u32[]{:S(2)}) copy-start(f32[768]{0:T(1024)} %convert_element_type.120) | copy-start | bytes 9220
  128.7 58.3 %copy-start.8 = (bf16[2,512,12,64]{1,0,3,2:T(2,128)(2,1)}, bf16[2,512,12,64]{1,0,3,2:T(2,128)(2,1)S(1)}, u32[]{:S(2)}) copy-start(bf16[2,512,12,64]{1,0,3,2:T(2,128)(2,1)S(1)} %reshape.171) | copy-start | bytes 4718596
  187.0 11.1 copy-start.6
  198.1 11.2 copy-start.11
  238.8 61.4 %copy-start.27 = (f32[3072]{0:T(1024)S(1)}, f32[3072]{0:T(1024)}, u32[]{:S(2)}) copy-start(f32[3072]{0:T(1024)} %convert_element_type.131) | copy-start | bytes 36868
  240.0 125.0 %copy-start.28 = (f32[768]{0:T(1024)S(1)}, f32[768]{0:T(1024)}, u32[]{:S(2)}) copy-start(f32[768]{0:T(1024)} %convert_element_type.133) | copy-start | bytes 9220
  374.2 1.9 copy-start.5
  374.2 1.9 copy-start.23
  376.1 1.6 copy-start.24
  411.5 1.6 copy-start.3
  411.5 3.1 copy-start.16
  413.5 1.2 copy-start.18
  424.3 4.0 copy-start.20
  424.3 4.0 copy-start.22
  428.2 202.8 %reduce-scatter.23.cloned.1.call-start = ((), (), s32[]{:S(2)}) async-start(), calls=%async_computation.17 | async-start | bytes 2433024
  440.2 3.2 copy-start.30
  442.3 1.2 copy-start.9
  469.3 266.2 %reduce-scatter.19.cloned.1.call-start = ((), (), s32[]{:S(2)}) async-start(), calls=%async_computation.15 | async-start | bytes 2433024
  469.4 18.2 %copy-start.7 = (bf16[2,512,12,64]{1,0,3,2:T(2,128)(2,1)S(1)}, bf16[2,512,12,64]{1,0,3,2:T(2,128)(2,1)}, u32[]{:S(2)}) copy-start(bf16[2,512,12,64]{1,0,3,2:T(2,128)(2,1)} %copy-done.6) | copy-start | bytes 4718596
  487.6 4.5 copy-start.2
  492.1 3.2 copy-start.31
  494.2 1.2 copy-start.12
  501.2 338.7 %reduce-scatter.21.cloned.1.call-start = ((), (), s32[]{:S(2)}) async-start(), calls=%async_computation.16 | async-start | bytes 2433024
  510.3 3.2 copy-start.32
  512.4 1.1 copy-start.14
  519.6 462.3 %reduce-scatter.15.cloned.1.call-start = ((), (), s32[]{:S(2)}) async-start(), calls=%async_computation.13 | async-start | bytes 9732096 | tf_op jit(solution)/shard_map/reduce_scatter | solution.py:166
  530.4 1.4 copy-start.17
  530.4 593.0 %reduce-scatter.17.cloned.1.call-start = ((), (), s32[]{:S(2)}) async-start(), calls=%async_computation.14 | async-start | bytes 9732096 | tf_op jit(solution)/shard_map/reduce_scatter | solution.py:168
  541.9 0.7 copy-start.25
  541.9 0.7 copy-start.26
  541.9 45.9 %copy-start.13 = (bf16[96,8,2,512]{3,1,2,0:T(8,128)(2,1)S(1)}, bf16[96,8,2,512]{3,1,2,0:T(8,128)(2,1)}, u32[]{:S(2)}) copy-start(bf16[96,8,2,512]{3,1,2,0:T(8,128)(2,1)} %copy-done.12) | copy-start | bytes 4718596
  541.9 45.9 %copy-start.33 = (bf16[768,768]{1,0:T(8,128)(2,1)S(1)}, bf16[768,768]{1,0:T(8,128)(2,1)}, u32[]{:S(2)}) copy-start(bf16[768,768]{1,0:T(8,128)(2,1)} %all-gather.9.cloned.1.call-done) | copy-start | bytes 3538948
  587.8 1.5 copy-start.15
  587.8 1.8 copy-start.34
  589.6 1.9 copy-start.4
  589.6 2.4 copy-start.10
  589.6 2.8 copy-start.19
  592.3 531.1 %copy-start.1 = (bf16[2,128,768]{2,1,0:T(8,128)(2,1)S(1)}, bf16[2,128,768]{2,1,0:T(8,128)(2,1)}, u32[]{:S(2)}) copy-start(bf16[2,128,768]{2,1,0:T(8,128)(2,1)} %param.22) | copy-start | bytes 1179652
Sparse Core Ops, SparseCore 0:
  10.9 56.8 all-gather.6
  70.7 52.8 all-gather.8
  126.5 52.8 all-gather.10
  182.1 52.8 all-gather.12
  237.7 62.4 all-gather.14
  303.0 61.9 all-gather.16
  428.3 97.9 reduce-scatter.12
  532.2 98.7 reduce-scatter.22
  636.9 98.6 reduce-scatter.18
  741.2 98.6 reduce-scatter.20
  846.4 135.4 reduce-scatter.14
  988.2 135.1 reduce-scatter.16
where the time goes:
time: 1140 us; the launch traced here: 1130 us
  waiting for transfers between devices  731 us (64%)
  matrix products  198 us (17%)
  blocking collectives  82.5 us (7%)
  local copies, waits for them, and re-layouts  61 us (5%)
  other arithmetic  42.6 us (4%)
  between operations  14.9 us (1%)
    unnamed x15, waiting for transfers between devices  248 us
    reduce_scatter x1, waiting for transfers between devices, body(): lax.psum_scatter(grad_up, ('fsdp', 'sub'), scatter_dimension=0, tiled=True)  142 us
    reduce_scatter x1, waiting for transfers between devices, body(): lax.psum_scatter(grad_down, ('fsdp', 'sub'), scatter_dimension=0, tiled=T...  142 us
    unnamed x2, blocking collectives  82.5 us
    all_gather x1, waiting for transfers between devices, body(): lax.all_gather(w_up, ('fsdp', 'sub'), axis=0, tiled=True)  60.2 us
    dot_general x6, matrix products, project(): return jnp.dot(rows_low, weight, preferred_element_type=jnp.float32)  58.3 us
    all_gather x1, waiting for transfers between devices, body(): lax.all_gather(w_key, ('fsdp', 'sub'), axis=0, tiled=True)  50.6 us
    all_gather x1, waiting for transfers between devices, body(): lax.all_gather(w_query, ('fsdp', 'sub'), axis=0, tiled=True)  48.7 us
  transfers between devices with their start and end apart: 12, of which 10 were waited for; matrix products, arithmetic and copies ran while one was open for 20% of the time, Pallas kernels for 0%

commit v1 on v0

v1 whole, which is shorter than its diff:
```python
import jax
import jax.numpy as jnp
from jax import lax
from jax.sharding import PartitionSpec as P

HD = 64
EPSILON = 1e-06
AXES = ("fsdp", "sub")
GRAD_WIRE = jnp.float32
VEC_COLS = 256


def layer_norm(values, gain, shift):
    average = jnp.mean(values, axis=-1, keepdims=True)
    centered = values - average
    variance = jnp.mean(centered * centered, axis=-1, keepdims=True)
    return centered * lax.rsqrt(variance + EPSILON) * gain + shift


def gelu_exact(values):
    return jax.nn.gelu(values, approximate=False)


def project(rows_low, weight):
    return jnp.dot(rows_low, weight, preferred_element_type=jnp.float32)


def reverse_projection(grad_low, weight):
    return lax.dot_general(
        grad_low, weight, (((1,), (1,)), ((), ())), preferred_element_type=jnp.float32
    )


def weight_grad(rows_low, grad_low):
    return lax.dot_general(
        rows_low, grad_low, (((0,), (0,)), ((), ())), preferred_element_type=jnp.float32
    )


def column_sum(grad_low):
    return jnp.sum(grad_low.astype(jnp.float32), axis=0)


def attention_scores(query_heads, key_heads, valid_keys, scale):
    scores = (
        jnp.einsum("sqhd,skhd->shqk", query_heads, key_heads, preferred_element_type=jnp.float32)
        * scale
    )
    return jnp.where(valid_keys[:, None, None, :], scores, -1e30)


def pack_vectors(rows, vectors, dtype):
    cols = [v.reshape(rows, -1).astype(dtype) for v in vectors]
    block = jnp.concatenate(cols, axis=1)
    return jnp.pad(block, ((0, 0), (0, VEC_COLS - block.shape[1])))


def unpack_vectors(block, widths):
    out, at = [], 0
    for width in widths:
        out.append(block[:, at : at + width].reshape(-1))
        at += width
    return out


def gather_rows(pack):
    return lax.all_gather(pack, AXES, axis=0, tiled=True)


def scatter_rows(pack):
    return lax.psum_scatter(pack.astype(GRAD_WIRE), AXES, scatter_dimension=0, tiled=True).astype(
        jnp.float32
    )


def body(
    inputs,
    lengths,
    positions,
    masked_output_gradient,
    w_query,
    b_query,
    w_key,
    w_value,
    b_value,
    w_out,
    b_out,
    gain_attn,
    shift_attn,
    w_up,
    b_up,
    w_down,
    b_down,
    gain_ffn,
    shift_ffn,
):
    seq_count, seq_slots, width = inputs.shape
    head_count = width // HD
    scale = HD ** (-0.5)
    row_count = seq_count * seq_slots
    head_shape = (seq_count, seq_slots, head_count, HD)
    shard_rows = w_query.shape[0]
    ff_ratio = w_down.shape[0] // shard_rows
    ff_width = w_up.shape[1]
    token_ids = jnp.arange(seq_slots, dtype=jnp.int32)
    valid_keys = token_ids[None, :] < lengths[:, None]

    with jax.named_scope("gather_attn"):
        attn_pack = jnp.concatenate(
            [
                w_query,
                w_key,
                w_value,
                w_out,
                pack_vectors(
                    shard_rows, (b_query, b_value, b_out, gain_attn, shift_attn), jnp.bfloat16
                ),
            ],
            axis=1,
        )
        attn_full = gather_rows(attn_pack)
    query_weight = attn_full[:, 0:width]
    key_weight = attn_full[:, width : 2 * width]
    value_weight = attn_full[:, 2 * width : 3 * width]
    out_weight = attn_full[:, 3 * width : 4 * width]
    query_bias, value_bias, out_bias, norm1_gain, norm1_shift = unpack_vectors(
        attn_full[:, 4 * width :], (1, 1, 1, 1, 1)
    )

    with jax.named_scope("gather_ffn"):
        ffn_pack = jnp.concatenate(
            [
                w_up,
                w_down.reshape(shard_rows, ff_ratio * width),
                pack_vectors(
                    shard_rows, (b_up, b_down, gain_ffn, shift_ffn), jnp.bfloat16
                ),
            ],
            axis=1,
        )
        ffn_full = gather_rows(ffn_pack)
    up_weight = ffn_full[:, 0:ff_width]
    down_weight = ffn_full[:, ff_width : 2 * ff_width].reshape(ff_width, width)
    up_bias, downward_bias, norm2_gain, norm2_shift = unpack_vectors(
        ffn_full[:, 2 * ff_width :], (ff_ratio, 1, 1, 1)
    )

    flat_in = inputs.reshape(row_count, width)
    input_rows = flat_in.astype(jnp.float32)
    query_low = (project(flat_in, query_weight) + query_bias.astype(jnp.float32)).astype(
        jnp.bfloat16
    )
    keys_low = project(flat_in, key_weight).astype(jnp.bfloat16)
    values_low = (project(flat_in, value_weight) + value_bias.astype(jnp.float32)).astype(
        jnp.bfloat16
    )
    query_heads = query_low.reshape(head_shape)
    key_heads = keys_low.reshape(head_shape)
    value_heads = values_low.reshape(head_shape)
    scores = attention_scores(query_heads, key_heads, valid_keys, scale)
    row_top = jnp.max(scores, axis=-1, keepdims=True)
    expon = jnp.exp(scores - row_top)
    row_total = jnp.sum(expon, axis=-1, keepdims=True)
    log_total = row_top + jnp.log(row_total)
    probs_low = (expon / row_total).astype(jnp.bfloat16)
    attention_mixed = jnp.einsum(
        "shqk,skhd->sqhd", probs_low, value_heads, preferred_element_type=jnp.float32
    )
    attended_low = attention_mixed.reshape(row_count, width).astype(jnp.bfloat16)
    branch = project(attended_low, out_weight) + out_bias.astype(jnp.float32)
    middle, norm1_pull = jax.vjp(
        layer_norm,
        input_rows + branch,
        norm1_gain.astype(jnp.float32),
        norm1_shift.astype(jnp.float32),
    )
    middle_low = middle.astype(jnp.bfloat16)
    hidden = project(middle_low, up_weight) + up_bias.astype(jnp.float32)
    active, gelu_pull = jax.vjp(gelu_exact, hidden)
    active_low = active.astype(jnp.bfloat16)
    second_branch = project(active_low, down_weight) + downward_bias.astype(jnp.float32)
    output, norm2_pull = jax.vjp(
        layer_norm,
        middle + second_branch,
        norm2_gain.astype(jnp.float32),
        norm2_shift.astype(jnp.float32),
    )
    position_matches = (positions[:, :, None] == token_ids[None, None, :]).astype(jnp.bfloat16)
    cotangent = jnp.einsum(
        "efw,efv->ewv", position_matches, masked_output_gradient, preferred_element_type=jnp.float32
    ).reshape(row_count, width)
    grad_sum2, grad_gain2, grad_shift2 = norm2_pull(cotangent)
    second_grad = grad_sum2.astype(jnp.bfloat16)
    grad_down = weight_grad(active_low, second_grad)
    grad_down_bias = column_sum(second_grad)
    (grad_hidden,) = gelu_pull(reverse_projection(second_grad, down_weight))
    hidden_grad = grad_hidden.astype(jnp.bfloat16)
    grad_up = weight_grad(middle_low, hidden_grad)
    grad_up_bias = column_sum(hidden_grad)
    grad_middle = grad_sum2 + reverse_projection(hidden_grad, up_weight)
    grad_residual, grad_gain1, grad_shift1 = norm1_pull(grad_middle)
    branch_grad = grad_residual.astype(jnp.bfloat16)
    grad_out = weight_grad(attended_low, branch_grad)
    grad_out_bias = column_sum(branch_grad)

    with jax.named_scope("scatter_late"):
        late_pack = jnp.concatenate(
            [
                grad_up,
                grad_down.reshape(width, ff_ratio * width),
                grad_out,
                pack_vectors(
                    width,
                    (
                        grad_up_bias,
                        grad_down_bias,
                        grad_gain2,
                        grad_shift2,
                        grad_out_bias,
                        grad_gain1,
                        grad_shift1,
                    ),
                    jnp.float32,
                ),
            ],
            axis=1,
        )
        late_own = scatter_rows(late_pack)
    grad_up_own = late_own[:, 0:ff_width]
    grad_down_own = late_own[:, ff_width : 2 * ff_width].reshape(shard_rows * ff_ratio, width)
    grad_out_own = late_own[:, 2 * ff_width : 2 * ff_width + width]
    (
        grad_up_bias_own,
        grad_down_bias_own,
        grad_gain2_own,
        grad_shift2_own,
        grad_out_bias_own,
        grad_gain1_own,
        grad_shift1_own,
    ) = unpack_vectors(late_own[:, 2 * ff_width + width :], (ff_ratio, 1, 1, 1, 1, 1, 1))

    attended_grad = (
        reverse_projection(branch_grad, out_weight).astype(jnp.bfloat16).reshape(head_shape)
    )
    scores_again = attention_scores(query_heads, key_heads, valid_keys, scale)
    probs = jnp.exp(scores_again - log_total)
    probs_again = probs.astype(jnp.bfloat16)
    probs_grad = jnp.einsum(
        "sqhd,skhd->shqk", attended_grad, value_heads, preferred_element_type=jnp.float32
    )
    values_grad = jnp.einsum(
        "shqk,sqhd->skhd", probs_again, attended_grad, preferred_element_type=jnp.float32
    )
    values_grad = values_grad.astype(jnp.bfloat16).reshape(row_count, width)
    inner_sum = jnp.sum(probs * probs_grad, axis=-1, keepdims=True)
    scores_grad = (probs * (probs_grad - inner_sum)).astype(jnp.bfloat16)
    query_grad = jnp.einsum(
        "shqk,skhd->sqhd", scores_grad, key_heads, preferred_element_type=jnp.float32
    )
    query_grad = (query_grad * scale).astype(jnp.bfloat16).reshape(row_count, width)
    keys_grad = jnp.einsum(
        "shqk,sqhd->skhd", scores_grad, query_heads, preferred_element_type=jnp.float32
    )
    keys_grad = (keys_grad * scale).astype(jnp.bfloat16).reshape(row_count, width)
    grad_query = weight_grad(flat_in, query_grad)
    grad_query_bias = column_sum(query_grad)
    grad_key = weight_grad(flat_in, keys_grad)
    grad_value = weight_grad(flat_in, values_grad)
    value_bias_gradient = column_sum(values_grad)
    grad_input = (
        grad_residual
        + reverse_projection(query_grad, query_weight)
        + reverse_projection(keys_grad, key_weight)
        + reverse_projection(values_grad, value_weight)
    )
    with jax.named_scope("scatter_qkv"):
        qkv_pack = jnp.concatenate(
            [
                grad_query,
                grad_key,
                grad_value,
                pack_vectors(width, (grad_query_bias, value_bias_gradient), jnp.float32),
            ],
            axis=1,
        )
        qkv_own = scatter_rows(qkv_pack)
    grad_query_own = qkv_own[:, 0:width]
    grad_key_own = qkv_own[:, width : 2 * width]
    grad_value_own = qkv_own[:, 2 * width : 3 * width]
    grad_query_bias_own, value_bias_gradient_own = unpack_vectors(
        qkv_own[:, 3 * width :], (1, 1)
    )
    return (
        output.astype(jnp.bfloat16).reshape(inputs.shape),
        grad_input.astype(jnp.bfloat16).reshape(inputs.shape),
        grad_query_own,
        grad_query_bias_own,
        grad_key_own,
        grad_value_own,
        value_bias_gradient_own,
        grad_out_own,
        grad_out_bias_own,
        grad_gain1_own,
        grad_shift1_own,
        grad_up_own,
        grad_up_bias_own,
        grad_down_own,
        grad_down_bias_own,
        grad_gain2_own,
        grad_shift2_own,
    )


def solution(mesh):
    rows3 = P(AXES, None, None)
    rows2 = P(AXES, None)
    rows1 = P(AXES)
    return jax.shard_map(
        body,
        mesh=mesh,
        in_specs=(
            rows3,
            rows1,
            rows2,
            rows3,
            rows2,
            rows1,
            rows2,
            rows2,
            rows1,
            rows2,
            rows1,
            rows1,
            rows1,
            rows2,
            rows1,
            rows2,
            rows1,
            rows1,
            rows1,
        ),
        out_specs=(
            rows3,
            rows3,
            rows2,
            rows1,
            rows2,
            rows2,
            rows1,
            rows2,
            rows1,
            rows1,
            rows1,
            rows2,
            rows1,
            rows2,
            rows1,
            rows1,
            rows1,
        ),
        check_vma=False,
    )
```

time: 1140 us -> 742 us (0.65)
  waiting for transfers between devices: 731 us -> 363 us
  blocking collectives: 82.5 us -> 0 us
  local copies, waits for them, and re-layouts: 61 us -> 94.4 us
  other arithmetic: 42.6 us -> 61.8 us
    unnamed x15 -> x5, waiting for transfers between devices: 248 us -> 58 us
    all_gather x6 -> x2, waiting for transfers between devices: 199 us -> 78.8 us  [gather_rows(): return lax.all_gather(pack, AXES, axis=0, tiled=True)]
    unnamed x2 -> x0, blocking collectives: 82.5 us -> none
    reduce_scatter x3 -> x1, waiting for transfers between devices: 283 us -> 226 us  [scatter_rows(): lax.psum_scatter(pack.astype(GRAD_WIRE), AXES, scatter_dimension=0, tiled...]
    reshape x1 -> x17, local copies, waits for them, and re-layouts: 3.87 us -> 34.2 us  [the longest x1 11.8 us: body(): grad_down.reshape(width, ff_ratio * width)]
    concatenate x0 -> x5, other arithmetic: none -> 14.3 us  [the longest x1 8.49 us: body(): jnp.concatenate([grad_up, grad_down.reshape(width, ff_ratio * width), gra...]
    slice x0 -> x7, local copies, waits for them, and re-layouts: none -> 13.1 us  [the longest x1 4.89 us: body(): down_weight = ffn_full[:, ff_width:2 * ff_width].reshape(ff_width, width)]
    unnamed x104 -> x85, local copies, waits for them, and re-layouts: 38.4 us -> 25.8 us
  transfers between devices with their start and end apart: 12 -> 4, of which waited for: 10 -> 4; matrix products, arithmetic and copies ran while one was open for 20% -> 19% of each run, Pallas kernels for 0% -> 0%
where the time goes in v1:
time: 742 us; the launch traced here: 737 us
  waiting for transfers between devices  363 us (49%)
  matrix products  204 us (27%)
  local copies, waits for them, and re-layouts  94.4 us (13%)
  other arithmetic  61.8 us (8%)
  between operations  14.6 us (2%)
    reduce_scatter x1, waiting for transfers between devices, scatter_rows(): lax.psum_scatter(pack.astype(GRAD_WIRE), AXES, scatter_dimension=0, tiled...  226 us
    all_gather x2, waiting for transfers between devices, gather_rows(): return lax.all_gather(pack, AXES, axis=0, tiled=True)  78.8 us
    unnamed x5, waiting for transfers between devices  58 us
    dot_general x6, matrix products, project(): return jnp.dot(rows_low, weight, preferred_element_type=jnp.float32)  57.6 us
    dot_general x6, matrix products, reverse_projection(): lax.dot_general(grad_low, weight, (((1,), (1,)), ((), ())), preferred_ele...  42.7 us
    dot_general x6, matrix products, weight_grad(): lax.dot_general(rows_low, grad_low, (((0,), (0,)), ((), ())), preferred_e...  28.4 us
    unnamed x85, local copies, waits for them, and re-layouts  25.8 us
    convert_element_type x1, other arithmetic, body(): scores_grad = (probs * (probs_grad - inner_sum)).astype(jnp.bfloat16)  21.6 us
  transfers between devices with their start and end apart: 4, of which 4 were waited for; matrix products, arithmetic and copies ran while one was open for 19% of the time, Pallas kernels for 0%

profile of v1, /device:TPU:0, one launch (start us, length us, event | category | flops | bytes accessed | tf_op | source)
XLA Modules:
  0.0 737.3 jit_solution(6974906823626849176)
XLA Ops:
  14.6 1.7 fusion.56
  17.2 3.5 fusion.75
  20.7 58.9 %all-gather.3.cloned.1.call-done = bf16[768,3328]{1,0:T(8,128)(2,1)} async-done(((bf16[24,3328]{1,0:T(8,128)(2,1)}), bf16[768,3328]{1,0:T(8,128)(2,1)}) %all-gather.3.cloned.1.call-update) | async-done | bytes 5111824 | tf_op jit(solution)/shard_map/gather_attn/all_gather | solution.py:67
  79.6 2.7 fusion.30
  82.3 1.5 reshape.339
  83.8 2.5 convert_reduce_fusion.9
  86.4 4.4 fusion.32
  90.8 2.9 reshape.338
  93.7 5.0 fusion.31
  98.7 3.8 reshape.337
  102.5 11.2 %fusion.12 = (f32[2,12,512]{2,1,0:T(8,128)S(1)}, f32[2,12,512,512]{2,3,1,0:T(8,128)}) fusion(pred[2,512]{1,0:T(4,128)(4,1)S(1)} %iota_compare_fusion.5, bf16[2,512,12,64]{1,0,3,2:T(2,128)(2,1)S(1)} %reshape.339, bf16[2,512,12,64]{1,0,3,2:T(2,128)(2,1)S(1)} %reshape.338), kind=kOutput, calls=%fused_computation.31 | convolution fusion | flops 824168448 | bytes 28361728 | tf_op jit(solution)/shard_map/sqhd,skhd->shqk/dot_general | solution.py:46
  113.7 11.2 %fusion = f32[2,12,512]{2,1,0:T(8,128)S(1)} fusion(f32[2,12,512]{2,1,0:T(8,128)S(1)} %get-tuple-element.122, f32[2,12,512,512]{2,3,1,0:T(8,128)} %get-tuple-element.123, pred[2,512]{1,0:T(4,128)(4,1)S(1)} %iota_compare_fusion.5), kind=kLoop, calls=%fused_computation.6 | loop fusion | flops 25153536 | bytes 25265152 | tf_op jit(solution)/shard_map/reduce_sum | solution.py:163
  124.9 13.3 %fusion.33 = bf16[2,512,12,64]{1,3,2,0:T(8,128)(2,1)S(1)} fusion(f32[2,12,512]{2,1,0:T(8,128)S(1)} %fusion, f32[2,12,512]{2,1,0:T(8,128)S(1)} %get-tuple-element.122, f32[2,12,512,512]{2,3,1,0:T(8,128)} %get-tuple-element.123, pred[2,512]{1,0:T(4,128)(4,1)S(1)} %iota_compare_fusion.5, bf16[2,512,12,64]{1,0,3,2:T(2,128)(2,1)S(1)} %copy-done.10), kind=kOutput, calls=%fused_computation.77 | convolution fusion | flops 837550080 | bytes 28410880 | tf_op jit(solution)/shard_map/shqk,skhd->sqhd/dot_general | solution.py:166
  138.2 1.6 copy.118
  140.3 3.5 fusion.73
  145.0 19.9 %all-gather.5.cloned.1.call-done = bf16[768,6400]{1,0:T(8,128)(2,1)} async-done(((bf16[24,6400]{1,0:T(8,128)(2,1)}), bf16[768,6400]{1,0:T(8,128)(2,1)}) %all-gather.5.cloned.1.call-update) | async-done | bytes 9830416 | tf_op jit(solution)/shard_map/gather_ffn/all_gather | solution.py:67
  166.6 4.9 slice.153
  171.5 8.5 %reshape.345 = bf16[3072,768]{1,0:T(8,128)(2,1)} reshape(bf16[768,3072]{1,0:T(8,128)(2,1)} %slice.153) | data formatting | bytes 9437184 | tf_op jit(solution)/shard_map/reshape | solution.py:143
  180.0 1.6 convert_reduce_fusion.6
  181.6 36.6 %multiply_convert_fusion.1 = (bf16[1024,3072]{1,0:T(8,128)(2,1)S(1)}, f32[1024,3072]{1,0:T(8,128)}, f32[1024,3072]{1,0:T(8,128)}) fusion(f32[3072]{0:T(1024)S(1)} %copy-done.28, bf16[768,6400]{1,0:T(8,128)(2,1)} %all-gather.5.cloned.1.call-done, f32[1024,768]{1,0:T(8,128)S(1)} %get-tuple-element.125, f32[768]{0:T(1024)S(1)} %get-tuple-element.93, ...), kind=kOutput, calls=%fused_computation.16 | convolution fusion | flops 5043388416 | bytes 39348224 | tf_op jit(solution)/shard_map/dot_general | solution.py:25
  218.2 5.4 fusion.74
  224.2 1.3 copy-done.4
  226.6 2.7 fusion.68
  229.4 1.5 convert_reduce_fusion.2
  230.8 18.5 %convert_reduce_fusion = (f32[3072]{0:T(1024)S(1)}, bf16[1024,3072]{1,0:T(8,128)(2,1)}) fusion(f32[1024,3072]{1,0:T(8,128)} %get-tuple-element.113, bf16[1024,768]{1,0:T(8,128)(2,1)} %get-tuple-element.107, bf16[3072,768]{1,0:T(8,128)(2,1)} %reshape.345, f32[1024,3072]{1,0:T(8,128)} %get-tuple-element.126, f32[3072]{0:T(1024)S(1)} %copy-done.28), kind=kOutput, calls=%fused_computation.13 | convolution fusion | flops 4885312512 | bytes 37773312 | tf_op jit(solution)/shard_map/dot_general | solution.py:29
  249.3 10.1 %multiply_reduce_fusion.1 = (f32[768]{0:T(1024)S(1)}, f32[1024]{0:T(1024)S(1)}, f32[768]{0:T(1024)S(1)}, f32[1024,768]{1,0:T(8,128)S(1)}) fusion(f32[1024,768]{1,0:T(8,128)S(1)} %get-tuple-element.125, f32[1024]{0:T(1024)S(1)} %fusion.58, f32[1024]{0:T(1024)S(1)} %broadcast_multiply_fusion.1, f32[768]{0:T(1024)S(1)} %get-tuple-element.92, ...), kind=kOutput, calls=%fused_computation.42 | convolution fusion | flops 4839699456 | bytes 20472832 | tf_op jit(solution)/shard_map/dot_general | solution.py:29
  259.5 1.5 fusion.67
  261.0 1.6 copy-done.2
  262.9 1.2 copy-done.18
  264.1 3.8 convolution_convert_fusion
  267.9 2.7 copy.121
  270.6 3.9 reshape.348
  274.5 19.9 %multiply_reduce_fusion = (f32[2,12,512]{2,1,0:T(8,128)S(1)}, f32[2,12,512,512]{2,3,1,0:T(8,128)}) fusion(f32[2,12,512]{2,1,0:T(8,128)S(1)} %copy-done.19, f32[2,12,512,512]{2,3,1,0:T(8,128)} %get-tuple-element.123, pred[2,512]{1,0:T(4,128)(4,1)S(1)} %copy-done.22, bf16[2,512,12,64]{1,0,3,2:T(2,128)(2,1)} %reshape.337, bf16[2,512,12,64]{1,0,3,2:T(2,128)(2,1)} %reshape.348), kind=kOutput, calls=%fused_computation.1 | convolution fusion | flops 836751360 | bytes 53576704 | tf_op jit(solution)/shard_map/sqhd,skhd->shqk/dot_general | solution.py:248
  294.4 21.6 %multiply_convert_fusion = bf16[2,12,512,512]{2,3,1,0:T(8,128)(2,1)} fusion(f32[2,12,512,512]{2,3,1,0:T(8,128)} %get-tuple-element.131, f32[2,12,512]{2,1,0:T(8,128)S(1)} %get-tuple-element.130, f32[2,12,512]{2,1,0:T(8,128)S(1)} %copy-done.19, f32[2,12,512,512]{2,3,1,0:T(8,128)} %get-tuple-element.123, pred[2,512]{1,0:T(4,128)(4,1)S(1)} %copy-done.22), kind=kLoop, calls=%fused_computation | loop fusion | flops 37748736 | bytes 63013888 | tf_op jit(solution)/shard_map/convert_element_type | solution.py:256
  316.0 8.6 %fusion.29 = bf16[2,512,12,64]{1,3,2,0:T(8,128)(2,1)S(1)} fusion(bf16[2,12,512,512]{2,3,1,0:T(8,128)(2,1)} %multiply_convert_fusion, bf16[2,512,12,64]{1,0,3,2:T(2,128)(2,1)S(1)} %copy-done.8), kind=kOutput, calls=%fused_computation.73 | convolution fusion | flops 806879232 | bytes 15728640 | tf_op jit(solution)/shard_map/shqk,sqhd->skhd/dot_general | solution.py:261
  324.6 6.9 convert_reduce_fusion.4
  331.5 11.6 %convert_reduce_fusion.3 = (f32[12,64]{1,0:T(8,128)S(1)}, bf16[2,512,12,64]{1,3,2,0:T(8,128)(2,1)S(1)}) fusion(f32[2,12,512]{2,1,0:T(8,128)S(1)} %copy-done.19, f32[2,12,512,512]{2,3,1,0:T(8,128)} %get-tuple-element.123, pred[2,512]{1,0:T(4,128)(4,1)S(1)} %copy-done.22, bf16[2,512,12,64]{1,0,3,2:T(2,128)(2,1)S(1)} %copy-done.11), kind=kOutput, calls=%fused_computation.45 | convolution fusion | flops 832830720 | bytes 28364800 | tf_op jit(solution)/shard_map/shqk,sqhd->skhd/dot_general | solution.py:251
  343.2 1.6 copy.129
  344.8 1.6 copy.159
  346.4 1.6 copy.126
  348.0 1.6 copy.158
  349.6 1.6 copy.132
  351.2 1.6 copy.160
  353.0 3.4 convolution_bitcast_fusion
  356.4 1.4 convolution_bitcast_fusion.1
  357.8 1.4 convolution_bitcast_fusion.2
  359.3 3.4 pad_maximum_fusion
  362.6 9.2 %copy.148 = f32[768,2560]{1,0:T(8,128)} copy(f32[768,2560]{0,1:T(8,128)} %pad_maximum_fusion) | data formatting | bytes 15728640
  379.2 10.4 %fusion.76 = f32[3072,768]{1,0:T(8,128)} fusion(bf16[1024,3072]{1,0:T(8,128)(2,1)} %copy-done.32, bf16[1024,768]{1,0:T(8,128)(2,1)} %get-tuple-element.107), kind=kOutput, calls=%fused_computation.152 | convolution fusion | flops 4831838208 | bytes 17301504 | tf_op jit(solution)/shard_map/dot_general | solution.py:35
  389.6 11.8 %reshape.357 = f32[768,3072]{1,0:T(8,128)} reshape(f32[3072,768]{1,0:T(8,128)} %fusion.76) | data formatting | bytes 18874368 | tf_op jit(solution)/shard_map/scatter_late/reshape | solution.py:210
  401.4 2.4 concatenate.30
  403.8 3.5 fusion.77
  407.4 8.2 %fusion.64 = f32[768,3072]{1,0:T(8,128)S(1)} fusion(bf16[1024,3072]{1,0:T(8,128)(2,1)} %get-tuple-element.137, f32[1024,768]{1,0:T(8,128)S(1)} %get-tuple-element.125, f32[768]{0:T(1024)S(1)} %copy-done.24, f32[768]{0:T(1024)S(1)} %get-tuple-element.92, f32[1024]{0:T(1024)S(1)} %fusion.58, f32[1024]{0:T(1024)S(1)} %broadcast_multiply_fusion.1), kind=kOutput, calls=%fused_computation.143 | convolution fusion | flops 4835770368 | bytes 18888704 | tf_op jit(solution)/shard_map/dot_general | solution.py:35
  415.6 8.5 %select_maximum_fusion = f32[768,7168]{1,0:T(8,128)} fusion(f32[768,10]{1,0:T(8,128)S(1)} %concatenate.30, f32[768,768]{1,0:T(8,128)S(1)} %fusion.77, f32[768,3072]{1,0:T(8,128)S(1)} %bitcast.100, f32[768,3072]{1,0:T(8,128)S(1)} %fusion.64), kind=kLoop, calls=%fused_computation.7 | loop fusion | flops 27525120 | bytes 43284480 | tf_op jit(solution)/shard_map/scatter_late/concatenate | solution.py:207
  424.2 1.4 copy-done.15
  425.6 2.8 fusion.46
  428.4 2.9 fusion.49
  431.4 4.5 add_convert_fusion.1
  435.9 57.9 %reduce-scatter.7.cloned.1.call-done = f32[24,2560]{1,0:T(8,128)} async-done(((f32[768,2560]{1,0:T(8,128)}), f32[24,2560]{1,0:T(8,128)}) %reduce-scatter.7.cloned.1.call-update) | async-done | bytes 245776
  495.8 1.6 fusion.72
  497.5 226.0 %reduce-scatter.5.cloned.1.call-done = f32[24,7168]{1,0:T(8,128)} async-done(((f32[768,7168]{1,0:T(8,128)}), f32[24,7168]{1,0:T(8,128)}) %reduce-scatter.5.cloned.1.call-update) | async-done | bytes 688144 | tf_op jit(solution)/shard_map/scatter_late/reduce_scatter | solution.py:71
  724.8 1.8 fusion.70
  727.4 1.5 slice.162
  728.9 1.7 slice_reduce_fusion
  (122 shorter events, 25.4 us)
Async XLA Ops:
  7.2 10.0 %copy-start = (bf16[2,128,768]{2,1,0:T(8,128)(2,1)S(1)}, bf16[2,128,768]{2,1,0:T(8,128)(2,1)}, u32[]{:S(2)}) copy-start(bf16[2,128,768]{2,1,0:T(8,128)(2,1)} %param.22) | copy-start | bytes 1179652
  7.2 72.4 %all-gather.3.cloned.1.call-start = ((), (), s32[]{:S(2)}) async-start(), calls=%async_computation.2 | async-start | bytes 5271552 | tf_op jit(solution)/shard_map/gather_attn/all_gather | solution.py:67
  11.2 0.7 copy-start.20
  11.9 152.9 %all-gather.5.cloned.1.call-start = ((), (), s32[]{:S(2)}) async-start(), calls=%async_computation.3 | async-start | bytes 10137600 | tf_op jit(solution)/shard_map/gather_ffn/all_gather | solution.py:67
  16.3 63.3 %copy-start.29 = (bf16[2,512,768]{2,1,0:T(8,128)(2,1)S(1)}, bf16[2,512,768]{2,1,0:T(8,128)(2,1)}, u32[]{:S(2)}) copy-start(bf16[2,512,768]{2,1,0:T(8,128)(2,1)} %param.19) | copy-start | bytes 4718596
  16.3 477.5 %reduce-scatter.7.cloned.1.call-start = ((), (), s32[]{:S(2)}) async-start(), calls=%async_computation.5 | async-start | bytes 8110080
  17.2 107.7 %copy-start.21 = (pred[2,512]{1,0:T(4,128)(4,1)}, pred[2,512]{1,0:T(4,128)(4,1)S(1)}, u32[]{:S(2)}) copy-start(pred[2,512]{1,0:T(4,128)(4,1)S(1)} %iota_compare_fusion.5) | copy-start | bytes 3076
  83.8 18.7 %copy-start.5 = (bf16[2,512,12,64]{1,0,3,2:T(2,128)(2,1)}, bf16[2,512,12,64]{1,0,3,2:T(2,128)(2,1)S(1)}, u32[]{:S(2)}) copy-start(bf16[2,512,12,64]{1,0,3,2:T(2,128)(2,1)S(1)} %reshape.339) | copy-start | bytes 4718596
  86.3 131.9 %copy-start.23 = (f32[768]{0:T(1024)}, f32[768]{0:T(1024)S(1)}, u32[]{:S(2)}) copy-start(f32[768]{0:T(1024)S(1)} %get-tuple-element.93) | copy-start | bytes 9220
  93.7 8.8 %copy-start.7 = (bf16[2,512,12,64]{1,0,3,2:T(2,128)(2,1)}, bf16[2,512,12,64]{1,0,3,2:T(2,128)(2,1)S(1)}, u32[]{:S(2)}) copy-start(bf16[2,512,12,64]{1,0,3,2:T(2,128)(2,1)S(1)} %reshape.338) | copy-start | bytes 4718596
  113.7 11.2 %copy-start.10 = (bf16[2,512,12,64]{1,0,3,2:T(2,128)(2,1)S(1)}, bf16[2,512,12,64]{1,0,3,2:T(2,128)(2,1)}, u32[]{:S(2)}) copy-start(bf16[2,512,12,64]{1,0,3,2:T(2,128)(2,1)} %reshape.337) | copy-start | bytes 4718596
  138.2 2.1 copy-start.30
  140.3 3.6 copy-start.13
  144.3 0.7 copy-start.25
  171.5 10.1 %copy-start.28 = (f32[3072]{0:T(1024)S(1)}, f32[3072]{0:T(1024)}, u32[]{:S(2)}) copy-start(f32[3072]{0:T(1024)} %reshape.378) | copy-start | bytes 36868
  181.6 36.6 %copy-start.12 = (bf16[3072,768]{1,0:T(8,128)(2,1)S(1)}, bf16[3072,768]{1,0:T(8,128)(2,1)}, u32[]{:S(2)}) copy-start(bf16[3072,768]{1,0:T(8,128)(2,1)} %reshape.345) | copy-start | bytes 14155780
  218.2 5.5 copy-start.32
  223.7 1.9 copy-start.4
  249.3 10.1 %copy-start.26 = (f32[1024]{0:T(1024)S(1)}, f32[1024]{0:T(1024)}, u32[]{:S(2)}) copy-start(f32[1024]{0:T(1024)} %copy-done.25) | copy-start | bytes 12292
  261.0 1.6 copy-start.2
  262.9 1.2 copy-start.18
  267.9 6.6 copy-start.19
  267.9 6.6 copy-start.22
  294.4 21.6 %copy-start.8 = (bf16[2,512,12,64]{1,0,3,2:T(2,128)(2,1)S(1)}, bf16[2,512,12,64]{1,0,3,2:T(2,128)(2,1)}, u32[]{:S(2)}) copy-start(bf16[2,512,12,64]{1,0,3,2:T(2,128)(2,1)} %copy-done.7) | copy-start | bytes 4718596
  316.0 8.6 %copy-start.6 = (bf16[2,512,12,64]{1,0,3,2:T(2,128)(2,1)S(1)}, bf16[2,512,12,64]{1,0,3,2:T(2,128)(2,1)}, u32[]{:S(2)}) copy-start(bf16[2,512,12,64]{1,0,3,2:T(2,128)(2,1)} %copy-done.5) | copy-start | bytes 4718596
  324.6 6.9 copy-start.11
  353.0 3.4 copy-start.14
  353.0 3.4 copy-start.31
  356.4 1.4 copy-start.16
  371.9 0.7 copy-start.27
  371.9 351.6 %reduce-scatter.5.cloned.1.call-start = ((), (), s32[]{:S(2)}) async-start(), calls=%async_computation.4 | async-start | bytes 22708224 | tf_op jit(solution)/shard_map/scatter_late/reduce_scatter | solution.py:71
  403.8 3.6 copy-start.24
  403.8 11.8 %slice-start = ((s8[9437184]{0:T(1024)(128)(4,1)}), s8[4194304]{0:T(1024)(128)(4,1)S(1)}, s32[]{:S(2)}) async-start(s8[9437184]{0:T(1024)(128)(4,1)} %bitcast.99), calls=%async_computation.6 | async-start | bytes 8388608
  407.4 8.3 %slice-start.1 = ((s8[9437184]{0:T(1024)(128)(4,1)}), s8[4194304]{0:T(1024)(128)(4,1)S(1)}, s32[]{:S(2)}) async-start(s8[9437184]{0:T(1024)(128)(4,1)} %bitcast.99), calls=%async_computation.7 | async-start | bytes 8388608
  407.4 8.3 %slice-start.2 = ((s8[9437184]{0:T(1024)(128)(4,1)}), s8[1048576]{0:T(1024)(128)(4,1)S(1)}, s32[]{:S(2)}) async-start(s8[9437184]{0:T(1024)(128)(4,1)} %bitcast.99), calls=%async_computation.8 | async-start | bytes 2097152
  424.1 1.4 copy-start.15
  425.6 2.9 copy-start.17
  428.4 2.9 copy-start.3
  428.4 2.9 copy-start.9
  431.3 299.3 %copy-start.1 = (bf16[2,128,768]{2,1,0:T(8,128)(2,1)S(1)}, bf16[2,128,768]{2,1,0:T(8,128)(2,1)}, u32[]{:S(2)}) copy-start(bf16[2,128,768]{2,1,0:T(8,128)(2,1)} %param.22) | copy-start | bytes 1179652
Sparse Core Ops, SparseCore 0:
  12.0 67.5 all-gather.2
  83.1 81.7 all-gather.4
  372.0 121.7 reduce-scatter.6
  500.1 223.3 reduce-scatter.4

commit v2 on v1

--- a/solution.py
+++ b/solution.py
@@ -225,6 +225,7 @@
             ],
             axis=1,
         )
+        late_pack, branch_grad = lax.optimization_barrier((late_pack, branch_grad))
         late_own = scatter_rows(late_pack)
     grad_up_own = late_own[:, 0:ff_width]
     grad_down_own = late_own[:, ff_width : 2 * ff_width].reshape(shard_rows * ff_ratio, width)
@@ -283,6 +284,7 @@
             ],
             axis=1,
         )
+        qkv_pack, late_own = lax.optimization_barrier((qkv_pack, late_own))
         qkv_own = scatter_rows(qkv_pack)
     grad_query_own = qkv_own[:, 0:width]
     grad_key_own = qkv_own[:, width : 2 * width]

time: 742 us -> 687 us (0.926)
  waiting for transfers between devices: 363 us -> 325 us
  matrix products: 204 us -> 193 us
  local copies, waits for them, and re-layouts: 94.4 us -> 84 us
    reduce_scatter x1, waiting for transfers between devices: 226 us -> 132 us  [scatter_rows(): lax.psum_scatter(pack.astype(GRAD_WIRE), AXES, scatter_dimension=0, tiled...]
    unnamed x5, waiting for transfers between devices: 58 us -> 109 us
    unnamed x85 -> x89, local copies, waits for them, and re-layouts: 25.8 us -> 23.7 us
  transfers between devices with their start and end apart: 4 -> 4, of which waited for: 4 -> 4; matrix products, arithmetic and copies ran while one was open for 19% -> 25% of each run, Pallas kernels for 0% -> 0%
where the time goes in v2:
time: 687 us; the launch traced here: 682 us
  waiting for transfers between devices  325 us (47%)
  matrix products  193 us (28%)
  local copies, waits for them, and re-layouts  84 us (12%)
  other arithmetic  65.8 us (10%)
  between operations  14.7 us (2%)
    reduce_scatter x1, waiting for transfers between devices, scatter_rows(): lax.psum_scatter(pack.astype(GRAD_WIRE), AXES, scatter_dimension=0, tiled...  132 us
    unnamed x5, waiting for transfers between devices  109 us
    all_gather x2, waiting for transfers between devices, gather_rows(): return lax.all_gather(pack, AXES, axis=0, tiled=True)  83.8 us
    dot_general x6, matrix products, project(): return jnp.dot(rows_low, weight, preferred_element_type=jnp.float32)  56.8 us
    dot_general x6, matrix products, reverse_projection(): lax.dot_general(grad_low, weight, (((1,), (1,)), ((), ())), preferred_ele...  39.7 us
    dot_general x6, matrix products, weight_grad(): lax.dot_general(rows_low, grad_low, (((0,), (0,)), ((), ())), preferred_e...  23.9 us
    unnamed x89, local copies, waits for them, and re-layouts  23.7 us
    dot_general x1, matrix products, body(): jnp.einsum('sqhd,skhd->shqk', attended_grad, value_heads, preferred_eleme...  21 us
  transfers between devices with their start and end apart: 4, of which 4 were waited for; matrix products, arithmetic and copies ran while one was open for 25% of the time, Pallas kernels for 0%

profile of v2, /device:TPU:0, one launch (start us, length us, event | category | flops | bytes accessed | tf_op | source)
XLA Modules:
  0.0 682.4 jit_solution(18305994713293535366)
XLA Ops:
  13.6 1.0 reshape.340
  14.7 1.7 fusion.56
  16.4 2.9 fusion.75
  19.3 0.9 reshape.384
  20.3 59.3 %all-gather.3.cloned.1.call-done = bf16[768,3328]{1,0:T(8,128)(2,1)} async-done(((bf16[24,3328]{1,0:T(8,128)(2,1)}), bf16[768,3328]{1,0:T(8,128)(2,1)}) %all-gather.3.cloned.1.call-update) | async-done | bytes 5111824 | tf_op jit(solution)/shard_map/gather_attn/all_gather | solution.py:67
  79.6 2.0 convert_reduce_fusion.9
  81.7 2.8 fusion.32
  84.5 1.4 reshape.338
  85.8 3.8 fusion.31
  89.7 2.4 reshape.337
  92.1 4.4 fusion.30
  96.4 2.9 reshape.339
  99.3 11.4 %fusion.12 = (f32[2,12,512]{2,1,0:T(8,128)S(1)}, f32[2,12,512,512]{2,3,1,0:T(8,128)}) fusion(pred[2,512]{1,0:T(4,128)(4,1)S(1)} %iota_compare_fusion.5, bf16[2,512,12,64]{1,0,3,2:T(2,128)(2,1)S(1)} %reshape.339, bf16[2,512,12,64]{1,0,3,2:T(2,128)(2,1)S(1)} %reshape.338), kind=kOutput, calls=%fused_computation.31 | convolution fusion | flops 824168448 | bytes 28361728 | tf_op jit(solution)/shard_map/sqhd,skhd->shqk/dot_general | solution.py:46
  110.7 11.2 %fusion = f32[2,12,512]{2,1,0:T(8,128)S(1)} fusion(f32[2,12,512]{2,1,0:T(8,128)S(1)} %get-tuple-element.128, f32[2,12,512,512]{2,3,1,0:T(8,128)} %get-tuple-element.129, pred[2,512]{1,0:T(4,128)(4,1)S(1)} %iota_compare_fusion.5), kind=kLoop, calls=%fused_computation.6 | loop fusion | flops 25153536 | bytes 25265152 | tf_op jit(solution)/shard_map/reduce_sum | solution.py:163
  121.9 11.6 %fusion.33 = bf16[2,512,12,64]{1,3,2,0:T(8,128)(2,1)S(1)} fusion(f32[2,12,512]{2,1,0:T(8,128)S(1)} %fusion, f32[2,12,512]{2,1,0:T(8,128)S(1)} %get-tuple-element.128, f32[2,12,512,512]{2,3,1,0:T(8,128)} %get-tuple-element.129, pred[2,512]{1,0:T(4,128)(4,1)S(1)} %iota_compare_fusion.5, bf16[2,512,12,64]{1,0,3,2:T(2,128)(2,1)S(1)} %copy-done.11), kind=kOutput, calls=%fused_computation.77 | convolution fusion | flops 837550080 | bytes 28410880 | tf_op jit(solution)/shard_map/shqk,skhd->sqhd/dot_general | solution.py:166
  133.6 1.6 copy.118
  135.7 3.6 fusion.73
  140.3 24.5 %all-gather.5.cloned.1.call-done = bf16[768,6400]{1,0:T(8,128)(2,1)} async-done(((bf16[24,6400]{1,0:T(8,128)(2,1)}), bf16[768,6400]{1,0:T(8,128)(2,1)}) %all-gather.5.cloned.1.call-update) | async-done | bytes 9830416 | tf_op jit(solution)/shard_map/gather_ffn/all_gather | solution.py:67
  164.8 1.0 slice_convert_fusion
  166.6 4.9 slice.153
  171.5 8.5 %reshape.345 = bf16[3072,768]{1,0:T(8,128)(2,1)} reshape(bf16[768,3072]{1,0:T(8,128)(2,1)} %slice.153) | data formatting | bytes 9437184 | tf_op jit(solution)/shard_map/reshape | solution.py:143
  180.0 1.6 convert_reduce_fusion.6
  181.6 36.9 %multiply_convert_fusion.1 = (bf16[1024,3072]{1,0:T(8,128)(2,1)S(1)}, f32[1024,3072]{1,0:T(8,128)}, f32[1024,3072]{1,0:T(8,128)}) fusion(f32[3072]{0:T(1024)S(1)} %copy-done.33, bf16[768,6400]{1,0:T(8,128)(2,1)} %all-gather.5.cloned.1.call-done, f32[1024,768]{1,0:T(8,128)S(1)} %get-tuple-element.131, f32[768]{0:T(1024)S(1)} %get-tuple-element.99, ...), kind=kOutput, calls=%fused_computation.16 | convolution fusion | flops 5043388416 | bytes 39348224 | tf_op jit(solution)/shard_map/dot_general | solution.py:25
  218.6 5.4 fusion.74
  224.5 1.3 copy-done.4
  225.9 1.0 fusion.17
  226.9 2.7 fusion.68
  229.7 0.9 reshape.383
  231.0 7.7 %fusion.76 = f32[3072,768]{1,0:T(8,128)} fusion(bf16[1024,3072]{1,0:T(8,128)(2,1)S(1)} %get-tuple-element.118, bf16[1024,768]{1,0:T(8,128)(2,1)S(1)} %get-tuple-element.115), kind=kOutput, calls=%fused_computation.152 | convolution fusion | flops 4831838208 | bytes 17301504 | tf_op jit(solution)/shard_map/dot_general | solution.py:35
  238.6 18.4 %convert_reduce_fusion = (f32[3072]{0:T(1024)S(1)}, bf16[1024,3072]{1,0:T(8,128)(2,1)}) fusion(f32[1024,3072]{1,0:T(8,128)} %get-tuple-element.119, bf16[1024,768]{1,0:T(8,128)(2,1)} %copy-done.22, bf16[3072,768]{1,0:T(8,128)(2,1)} %reshape.345, f32[1024,3072]{1,0:T(8,128)} %get-tuple-element.132, f32[3072]{0:T(1024)S(1)} %copy-done.33), kind=kOutput, calls=%fused_computation.13 | convolution fusion | flops 4885312512 | bytes 37773312 | tf_op jit(solution)/shard_map/dot_general | solution.py:29
  257.0 10.7 %fusion.64 = f32[768,3072]{1,0:T(8,128)} fusion(bf16[1024,3072]{1,0:T(8,128)(2,1)} %get-tuple-element.136, f32[1024,768]{1,0:T(8,128)S(1)} %get-tuple-element.131, f32[768]{0:T(1024)S(1)} %get-tuple-element.99, f32[768]{0:T(1024)S(1)} %get-tuple-element.98, f32[1024]{0:T(1024)S(1)} %fusion.58, f32[1024]{0:T(1024)S(1)} %broadcast_multiply_fusion.1), kind=kOutput, calls=%fused_computation.143 | convolution fusion | flops 4835770368 | bytes 18888704 | tf_op jit(solution)/shard_map/dot_general | solution.py:35
  267.7 8.4 %multiply_reduce_fusion.1 = (f32[768]{0:T(1024)S(1)}, f32[1024]{0:T(1024)S(1)}, f32[768]{0:T(1024)S(1)}, f32[1024,768]{1,0:T(8,128)S(1)}) fusion(f32[1024,768]{1,0:T(8,128)S(1)} %get-tuple-element.131, f32[1024]{0:T(1024)S(1)} %fusion.58, f32[1024]{0:T(1024)S(1)} %broadcast_multiply_fusion.1, f32[768]{0:T(1024)S(1)} %get-tuple-element.98, ...), kind=kOutput, calls=%fused_computation.47 | convolution fusion | flops 4839699456 | bytes 20472832 | tf_op jit(solution)/shard_map/dot_general | solution.py:29
  276.1 2.9 fusion.67
  279.0 1.2 reshape.349
  281.1 0.9 reshape.382
  282.9 2.2 convert_reduce_fusion.3
  285.2 1.1 reshape.385
  286.5 1.4 fusion.77
  287.9 11.6 %reshape.348 = f32[768,3072]{1,0:T(8,128)} reshape(f32[3072,768]{1,0:T(8,128)} %fusion.76) | data formatting | bytes 18874368 | tf_op jit(solution)/shard_map/scatter_late/reshape | solution.py:210
  299.4 2.1 concatenate.28
  301.5 14.8 %select_maximum_fusion = f32[768,7168]{1,0:T(8,128)} fusion(f32[768,10]{1,0:T(8,128)S(1)} %concatenate.28, f32[768,768]{1,0:T(8,128)S(1)} %fusion.77, f32[768,3072]{1,0:T(8,128)} %reshape.348, f32[768,3072]{1,0:T(8,128)} %fusion.64), kind=kLoop, calls=%fused_computation.7 | loop fusion | flops 27525120 | bytes 43284480 | tf_op jit(solution)/shard_map/scatter_late/concatenate | solution.py:207
  317.8 2.7 convolution_convert_fusion
  321.3 1.2 reshape.356
  322.5 14.9 %convert_reduce_fusion.1 = (f32[12,64]{1,0:T(8,128)S(1)}, bf16[2,512,12,64]{1,3,2,0:T(8,128)(2,1)}) fusion(f32[2,12,512]{2,1,0:T(8,128)S(1)} %log_add_fusion, f32[2,12,512,512]{2,3,1,0:T(8,128)} %get-tuple-element.129, pred[2,512]{1,0:T(4,128)(4,1)S(1)} %copy-done.30, bf16[2,512,12,64]{1,0,3,2:T(2,128)(2,1)S(1)} %reshape.356), kind=kOutput, calls=%fused_computation.42 | convolution fusion | flops 832830720 | bytes 28364800 | tf_op jit(solution)/shard_map/shqk,sqhd->skhd/dot_general | solution.py:252
  337.5 3.3 copy.139
  340.8 1.6 copy.160
  342.4 21.0 %multiply_reduce_fusion = (f32[2,12,512]{2,1,0:T(8,128)S(1)}, f32[2,12,512,512]{2,3,1,0:T(8,128)}) fusion(f32[2,12,512]{2,1,0:T(8,128)S(1)} %log_add_fusion, f32[2,12,512,512]{2,3,1,0:T(8,128)} %get-tuple-element.129, pred[2,512]{1,0:T(4,128)(4,1)S(1)} %copy-done.30, bf16[2,512,12,64]{1,0,3,2:T(2,128)(2,1)S(1)} %copy-done.12, ...), kind=kOutput, calls=%fused_computation.1 | convolution fusion | flops 836751360 | bytes 53576704 | tf_op jit(solution)/shard_map/sqhd,skhd->shqk/dot_general | solution.py:249
  363.4 18.9 %multiply_convert_fusion = bf16[2,12,512,512]{2,3,1,0:T(8,128)(2,1)S(1)} fusion(f32[2,12,512,512]{2,3,1,0:T(8,128)} %get-tuple-element.141, f32[2,12,512]{2,1,0:T(8,128)S(1)} %get-tuple-element.140, f32[2,12,512]{2,1,0:T(8,128)S(1)} %log_add_fusion, f32[2,12,512,512]{2,3,1,0:T(8,128)} %get-tuple-element.129, pred[2,512]{1,0:T(4,128)(4,1)S(1)} %copy-done.30), kind=kLoop, calls=%fused_computation | loop fusion | flops 37748736 | bytes 63013888 | tf_op jit(solution)/shard_map/convert_element_type | solution.py:257
  382.3 2.2 convert_reduce_fusion.2
  384.5 2.5 copy-done.2
  387.2 8.5 %fusion.29 = bf16[2,512,12,64]{1,3,2,0:T(8,128)(2,1)S(1)} fusion(bf16[2,12,512,512]{2,3,1,0:T(8,128)(2,1)} %copy-done.2, bf16[2,512,12,64]{1,0,3,2:T(2,128)(2,1)S(1)} %copy-done.8), kind=kOutput, calls=%fused_computation.73 | convolution fusion | flops 806879232 | bytes 15728640 | tf_op jit(solution)/shard_map/shqk,sqhd->skhd/dot_general | solution.py:262
  395.7 1.6 copy.136
  397.8 1.6 copy.133
  400.2 1.4 convolution_bitcast_fusion
  401.6 1.4 convolution_bitcast_fusion.2
  403.0 1.4 convolution_bitcast_fusion.1
  404.4 3.6 pad_maximum_fusion
  408.0 131.6 %reduce-scatter.5.cloned.1.call-done = f32[24,7168]{1,0:T(8,128)} async-done(((f32[768,7168]{1,0:T(8,128)}), f32[24,7168]{1,0:T(8,128)}) %reduce-scatter.5.cloned.1.call-update) | async-done | bytes 688144 | tf_op jit(solution)/shard_map/scatter_late/reduce_scatter | solution.py:71
  539.5 9.3 %copy.148 = f32[768,2560]{1,0:T(8,128)} copy(f32[768,2560]{0,1:T(8,128)} %pad_maximum_fusion) | data formatting | bytes 15728640
  548.9 2.9 fusion.49
  551.8 2.9 fusion.46
  554.7 4.6 add_convert_fusion.1
  562.9 109.1 %reduce-scatter.7.cloned.1.call-done = f32[24,2560]{1,0:T(8,128)} async-done(((f32[768,2560]{1,0:T(8,128)}), f32[24,2560]{1,0:T(8,128)}) %reduce-scatter.7.cloned.1.call-update) | async-done | bytes 245776
  674.0 1.6 fusion.72
  (126 shorter events, 21.0 us)
Async XLA Ops:
  7.2 9.2 %copy-start = (bf16[2,128,768]{2,1,0:T(8,128)(2,1)S(1)}, bf16[2,128,768]{2,1,0:T(8,128)(2,1)}, u32[]{:S(2)}) copy-start(bf16[2,128,768]{2,1,0:T(8,128)(2,1)} %param.22) | copy-start | bytes 1179652
  7.2 13.0 %copy-start.34 = (s32[2]{0:T(128)S(1)}, s32[2]{0:T(128)}, u32[]{:S(2)}) copy-start(s32[2]{0:T(128)} %param.20) | copy-start | bytes 28
  7.2 72.4 %all-gather.3.cloned.1.call-start = ((), (), s32[]{:S(2)}) async-start(), calls=%async_computation.2 | async-start | bytes 5271552 | tf_op jit(solution)/shard_map/gather_attn/all_gather | solution.py:67
  11.2 0.7 copy-start.28
  11.2 70.4 %copy-start.35 = (bf16[2,512,768]{2,1,0:T(8,128)(2,1)S(1)}, bf16[2,512,768]{2,1,0:T(8,128)(2,1)}, u32[]{:S(2)}) copy-start(bf16[2,512,768]{2,1,0:T(8,128)(2,1)} %param.19) | copy-start | bytes 4718596
  11.9 152.9 %all-gather.5.cloned.1.call-start = ((), (), s32[]{:S(2)}) async-start(), calls=%async_computation.3 | async-start | bytes 10137600 | tf_op jit(solution)/shard_map/gather_ffn/all_gather | solution.py:67
  16.3 523.2 %reduce-scatter.5.cloned.1.call-start = ((), (), s32[]{:S(2)}) async-start(), calls=%async_computation.4 | async-start | bytes 22708224 | tf_op jit(solution)/shard_map/scatter_late/reduce_scatter | solution.py:71
  20.3 101.6 %copy-start.29 = (pred[2,512]{1,0:T(4,128)(4,1)}, pred[2,512]{1,0:T(4,128)(4,1)S(1)}, u32[]{:S(2)}) copy-start(pred[2,512]{1,0:T(4,128)(4,1)S(1)} %iota_compare_fusion.5) | copy-start | bytes 3076
  85.8 13.5 %copy-start.7 = (bf16[2,512,12,64]{1,0,3,2:T(2,128)(2,1)}, bf16[2,512,12,64]{1,0,3,2:T(2,128)(2,1)S(1)}, u32[]{:S(2)}) copy-start(bf16[2,512,12,64]{1,0,3,2:T(2,128)(2,1)S(1)} %reshape.338) | copy-start | bytes 4718596
  99.3 11.4 %copy-start.5 = (bf16[2,512,12,64]{1,0,3,2:T(2,128)(2,1)}, bf16[2,512,12,64]{1,0,3,2:T(2,128)(2,1)S(1)}, u32[]{:S(2)}) copy-start(bf16[2,512,12,64]{1,0,3,2:T(2,128)(2,1)S(1)} %reshape.339) | copy-start | bytes 4718596
  110.7 11.2 %copy-start.24 = (f32[2,12,512]{2,1,0:T(8,128)}, f32[2,12,512]{2,1,0:T(8,128)S(1)}, u32[]{:S(2)}) copy-start(f32[2,12,512]{2,1,0:T(8,128)S(1)} %get-tuple-element.128) | copy-start | bytes 147460
  110.7 11.2 %copy-start.11 = (bf16[2,512,12,64]{1,0,3,2:T(2,128)(2,1)S(1)}, bf16[2,512,12,64]{1,0,3,2:T(2,128)(2,1)}, u32[]{:S(2)}) copy-start(bf16[2,512,12,64]{1,0,3,2:T(2,128)(2,1)} %reshape.337) | copy-start | bytes 4718596
  121.9 11.7 %copy-start.26 = (f32[2,12,512]{2,1,0:T(8,128)}, f32[2,12,512]{2,1,0:T(8,128)S(1)}, u32[]{:S(2)}) copy-start(f32[2,12,512]{2,1,0:T(8,128)S(1)} %fusion) | copy-start | bytes 147460
  133.6 2.1 copy-start.36
  135.7 3.6 copy-start.14
  139.7 0.6 copy-start.31
  171.5 10.1 %copy-start.33 = (f32[3072]{0:T(1024)S(1)}, f32[3072]{0:T(1024)}, u32[]{:S(2)}) copy-start(f32[3072]{0:T(1024)} %reshape.378) | copy-start | bytes 36868
  181.6 36.9 %copy-start.13 = (bf16[3072,768]{1,0:T(8,128)(2,1)S(1)}, bf16[3072,768]{1,0:T(8,128)(2,1)}, u32[]{:S(2)}) copy-start(bf16[3072,768]{1,0:T(8,128)(2,1)} %reshape.345) | copy-start | bytes 14155780
  224.0 1.9 copy-start.4
  231.0 7.7 %copy-start.22 = (bf16[1024,768]{1,0:T(8,128)(2,1)}, bf16[1024,768]{1,0:T(8,128)(2,1)S(1)}, u32[]{:S(2)}) copy-start(bf16[1024,768]{1,0:T(8,128)(2,1)S(1)} %get-tuple-element.115) | copy-start | bytes 4718596
  257.0 10.7 %copy-start.9 = (bf16[1024,3072]{1,0:T(8,128)(2,1)S(1)}, bf16[1024,3072]{1,0:T(8,128)(2,1)}, u32[]{:S(2)}) copy-start(bf16[1024,3072]{1,0:T(8,128)(2,1)} %get-tuple-element.136) | copy-start | bytes 18874372
  267.7 8.4 %copy-start.32 = (f32[1024]{0:T(1024)S(1)}, f32[1024]{0:T(1024)}, u32[]{:S(2)}) copy-start(f32[1024]{0:T(1024)} %copy-done.31) | copy-start | bytes 12292
  280.2 6.3 copy-start.15
  285.2 1.3 copy-start.20
  287.8 11.6 %copy-start.18 = (f32[768,1]{1,0:T(8,128)S(1)}, f32[768,1]{1,0:T(8,128)}, u32[]{:S(2)}) copy-start(f32[768,1]{1,0:T(8,128)} %reshape.384) | copy-start | bytes 9220
  287.9 11.6 %copy-start.19 = (f32[768,1]{1,0:T(8,128)S(1)}, f32[768,1]{1,0:T(8,128)}, u32[]{:S(2)}) copy-start(f32[768,1]{1,0:T(8,128)} %reshape.383) | copy-start | bytes 9220
  316.3 0.8 copy-start.25
  316.3 0.9 copy-start.27
  316.3 1.5 copy-start.21
  316.4 355.6 %reduce-scatter.7.cloned.1.call-start = ((), (), s32[]{:S(2)}) async-start(), calls=%async_computation.5 | async-start | bytes 8110080
  320.5 2.0 copy-start.30
  337.5 4.9 copy-start.12
  363.4 18.9 %copy-start.6 = (bf16[2,512,12,64]{1,0,3,2:T(2,128)(2,1)S(1)}, bf16[2,512,12,64]{1,0,3,2:T(2,128)(2,1)}, u32[]{:S(2)}) copy-start(bf16[2,512,12,64]{1,0,3,2:T(2,128)(2,1)} %copy-done.5) | copy-start | bytes 4718596
  382.3 4.8 copy-start.2
  382.3 4.9 copy-start.8
  397.7 5.3 copy-start.16
  397.7 2.1 copy-start.10
  397.7 2.5 copy-start.37
  548.9 2.9 copy-start.17
  551.8 2.9 copy-start.3
  554.7 4.6 slice-start
  554.7 5.2 copy-start.23
  554.7 121.0 %copy-start.1 = (bf16[2,128,768]{2,1,0:T(8,128)(2,1)S(1)}, bf16[2,128,768]{2,1,0:T(8,128)(2,1)}, u32[]{:S(2)}) copy-start(bf16[2,128,768]{2,1,0:T(8,128)(2,1)} %param.22) | copy-start | bytes 1179652
Sparse Core Ops, SparseCore 0:
  12.0 67.5 all-gather.2
  83.1 81.6 all-gather.4
  316.5 223.0 reduce-scatter.4
  549.0 122.9 reduce-scatter.6

commit v3 on v2

--- a/solution.py
+++ b/solution.py
@@ -6,7 +6,7 @@
 HD = 64
 EPSILON = 1e-06
 AXES = ("fsdp", "sub")
-GRAD_WIRE = jnp.float32
+GRAD_WIRE = jnp.bfloat16
 VEC_COLS = 256
 
 

time: 687 us -> 575 us (0.84)
  waiting for transfers between devices: 325 us -> 207 us
  matrix products: 193 us -> 200 us
    reduce_scatter x1, waiting for transfers between devices: 132 us -> 39.6 us  [scatter_rows(): lax.psum_scatter(pack.astype(GRAD_WIRE), AXES, scatter_dimension=0, tiled...]
    unnamed x5, waiting for transfers between devices: 109 us -> 88.6 us
  transfers between devices with their start and end apart: 4 -> 4, of which waited for: 4 -> 4; matrix products, arithmetic and copies ran while one was open for 25% -> 33% of each run, Pallas kernels for 0% -> 0%
where the time goes in v3:
time: 575 us; the launch traced here: 571 us
  waiting for transfers between devices  207 us (36%)
  matrix products  200 us (35%)
  local copies, waits for them, and re-layouts  83.7 us (15%)
  other arithmetic  64.8 us (11%)
  between operations  14.8 us (3%)
    unnamed x5, waiting for transfers between devices  88.6 us
    all_gather x2, waiting for transfers between devices, gather_rows(): return lax.all_gather(pack, AXES, axis=0, tiled=True)  78.5 us
    dot_general x6, matrix products, project(): return jnp.dot(rows_low, weight, preferred_element_type=jnp.float32)  58.1 us
    dot_general x6, matrix products, reverse_projection(): lax.dot_general(grad_low, weight, (((1,), (1,)), ((), ())), preferred_ele...  40.7 us
    reduce_scatter x1, waiting for transfers between devices, scatter_rows(): lax.psum_scatter(pack.astype(GRAD_WIRE), AXES, scatter_dimension=0, tiled...  39.6 us
    dot_general x6, matrix products, weight_grad(): lax.dot_general(rows_low, grad_low, (((0,), (0,)), ((), ())), preferred_e...  25.7 us
    unnamed x89, local copies, waits for them, and re-layouts  24 us
    convert_element_type x1, other arithmetic, body(): scores_grad = (probs * (probs_grad - inner_sum)).astype(jnp.bfloat16)  23.9 us
  transfers between devices with their start and end apart: 4, of which 4 were waited for; matrix products, arithmetic and copies ran while one was open for 33% of the time, Pallas kernels for 0%

profile of v3, /device:TPU:0, one launch (start us, length us, event | category | flops | bytes accessed | tf_op | source)
XLA Modules:
  0.0 570.8 jit_solution(8367692808856772535)
XLA Ops:
  13.6 1.0 reshape.340
  14.7 1.7 fusion.56
  16.4 2.9 fusion.74
  20.2 59.4 %all-gather.3.cloned.1.call-done = bf16[768,3328]{1,0:T(8,128)(2,1)} async-done(((bf16[24,3328]{1,0:T(8,128)(2,1)}), bf16[768,3328]{1,0:T(8,128)(2,1)}) %all-gather.3.cloned.1.call-update) | async-done | bytes 5111824 | tf_op jit(solution)/shard_map/gather_attn/all_gather | solution.py:67
  79.6 3.2 fusion.30
  82.8 1.5 reshape.339
  84.3 2.5 convert_reduce_fusion.9
  86.8 4.4 fusion.32
  91.2 2.9 reshape.338
  94.1 5.0 fusion.31
  99.1 3.9 reshape.337
  103.0 11.1 %fusion.12 = (f32[2,12,512]{2,1,0:T(8,128)S(1)}, f32[2,12,512,512]{2,3,1,0:T(8,128)}) fusion(pred[2,512]{1,0:T(4,128)(4,1)S(1)} %iota_compare_fusion.5, bf16[2,512,12,64]{1,0,3,2:T(2,128)(2,1)S(1)} %reshape.339, bf16[2,512,12,64]{1,0,3,2:T(2,128)(2,1)S(1)} %reshape.338), kind=kOutput, calls=%fused_computation.31 | convolution fusion | flops 824168448 | bytes 28361728 | tf_op jit(solution)/shard_map/sqhd,skhd->shqk/dot_general | solution.py:46
  114.1 11.2 %fusion = f32[2,12,512]{2,1,0:T(8,128)S(1)} fusion(f32[2,12,512]{2,1,0:T(8,128)S(1)} %get-tuple-element.128, f32[2,12,512,512]{2,3,1,0:T(8,128)} %get-tuple-element.129, pred[2,512]{1,0:T(4,128)(4,1)S(1)} %iota_compare_fusion.5), kind=kLoop, calls=%fused_computation.6 | loop fusion | flops 25153536 | bytes 25265152 | tf_op jit(solution)/shard_map/reduce_sum | solution.py:163
  125.4 13.1 %fusion.33 = bf16[2,512,12,64]{1,3,2,0:T(8,128)(2,1)S(1)} fusion(f32[2,12,512]{2,1,0:T(8,128)S(1)} %fusion, f32[2,12,512]{2,1,0:T(8,128)S(1)} %get-tuple-element.128, f32[2,12,512,512]{2,3,1,0:T(8,128)} %get-tuple-element.129, pred[2,512]{1,0:T(4,128)(4,1)S(1)} %iota_compare_fusion.5, bf16[2,512,12,64]{1,0,3,2:T(2,128)(2,1)S(1)} %copy-done.11), kind=kOutput, calls=%fused_computation.77 | convolution fusion | flops 837550080 | bytes 28410880 | tf_op jit(solution)/shard_map/shqk,skhd->sqhd/dot_general | solution.py:166
  138.5 1.6 copy.118
  140.6 3.5 fusion.72
  144.7 1.0 copy-done.29
  145.6 19.2 %all-gather.5.cloned.1.call-done = bf16[768,6400]{1,0:T(8,128)(2,1)} async-done(((bf16[24,6400]{1,0:T(8,128)(2,1)}), bf16[768,6400]{1,0:T(8,128)(2,1)}) %all-gather.5.cloned.1.call-update) | async-done | bytes 9830416 | tf_op jit(solution)/shard_map/gather_ffn/all_gather | solution.py:67
  166.6 4.9 slice.153
  171.5 8.5 %reshape.345 = bf16[3072,768]{1,0:T(8,128)(2,1)} reshape(bf16[768,3072]{1,0:T(8,128)(2,1)} %slice.153) | data formatting | bytes 9437184 | tf_op jit(solution)/shard_map/reshape | solution.py:143
  179.9 1.6 convert_reduce_fusion.6
  181.6 36.5 %multiply_convert_fusion.1 = (bf16[1024,3072]{1,0:T(8,128)(2,1)S(1)}, f32[1024,3072]{1,0:T(8,128)}, f32[1024,3072]{1,0:T(8,128)}) fusion(f32[3072]{0:T(1024)S(1)} %copy-done.31, bf16[768,6400]{1,0:T(8,128)(2,1)} %all-gather.5.cloned.1.call-done, f32[1024,768]{1,0:T(8,128)S(1)} %get-tuple-element.131, f32[768]{0:T(1024)S(1)} %get-tuple-element.99, ...), kind=kOutput, calls=%fused_computation.16 | convolution fusion | flops 5043388416 | bytes 39348224 | tf_op jit(solution)/shard_map/dot_general | solution.py:25
  218.1 5.4 fusion.73
  224.1 1.3 copy-done.2
  225.5 1.0 fusion.17
  226.5 2.7 fusion.68
  229.2 1.7 copy-done.8
  231.3 7.0 %fusion.75 = bf16[3072,768]{1,0:T(8,128)(2,1)} fusion(bf16[1024,3072]{1,0:T(8,128)(2,1)S(1)} %get-tuple-element.118, bf16[1024,768]{1,0:T(8,128)(2,1)S(1)} %get-tuple-element.115), kind=kOutput, calls=%fused_computation.153 | convolution fusion | flops 4831838208 | bytes 12582912 | tf_op jit(solution)/shard_map/dot_general | solution.py:35
  238.3 17.1 %convert_reduce_fusion = (bf16[3072]{0:T(1024)(128)(2,1)S(1)}, bf16[1024,3072]{1,0:T(8,128)(2,1)}) fusion(f32[1024,3072]{1,0:T(8,128)} %get-tuple-element.119, bf16[1024,768]{1,0:T(8,128)(2,1)S(1)} %get-tuple-element.115, bf16[3072,768]{1,0:T(8,128)(2,1)} %reshape.345, f32[1024,3072]{1,0:T(8,128)} %get-tuple-element.132, f32[3072]{0:T(1024)S(1)} %copy-done.31), kind=kOutput, calls=%fused_computation.13 | convolution fusion | flops 4885312512 | bytes 37767168 | tf_op jit(solution)/shard_map/dot_general | solution.py:29
  255.4 1.1 reshape.349
  258.3 10.0 %fusion.64 = bf16[768,3072]{1,0:T(8,128)(2,1)} fusion(bf16[1024,3072]{1,0:T(8,128)(2,1)} %get-tuple-element.136, f32[1024,768]{1,0:T(8,128)S(1)} %get-tuple-element.131, f32[768]{0:T(1024)S(1)} %get-tuple-element.99, f32[768]{0:T(1024)S(1)} %get-tuple-element.98, f32[1024]{0:T(1024)S(1)} %fusion.58, f32[1024]{0:T(1024)S(1)} %broadcast_multiply_fusion.1), kind=kOutput, calls=%fused_computation.145 | convolution fusion | flops 4835770368 | bytes 14170112 | tf_op jit(solution)/shard_map/dot_general | solution.py:35
  268.3 8.4 %multiply_reduce_fusion.1 = (bf16[768]{0:T(1024)(128)(2,1)S(1)}, f32[1024]{0:T(1024)S(1)}, bf16[768]{0:T(1024)(128)(2,1)S(1)}, f32[1024,768]{1,0:T(8,128)S(1)}) fusion(f32[1024,768]{1,0:T(8,128)S(1)} %get-tuple-element.131, f32[1024]{0:T(1024)S(1)} %fusion.58, f32[1024]{0:T(1024)S(1)} %broadcast_multiply_fusion.1, f32[768]{0:T(1024)S(1)} %get-tuple-element.98, ...), kind=kOutput, calls=%fused_computation.47 | convolution fusion | flops 4839699456 | bytes 20469760 | tf_op jit(solution)/shard_map/dot_general | solution.py:29
  276.7 3.0 fusion.67
  282.7 2.4 fusion.76
  285.1 8.5 %reshape.348 = bf16[768,3072]{1,0:T(8,128)(2,1)} reshape(bf16[3072,768]{1,0:T(8,128)(2,1)} %fusion.75) | data formatting | bytes 9437184 | tf_op jit(solution)/shard_map/scatter_late/reshape | solution.py:210
  293.7 1.7 concatenate.28
  295.4 9.5 %select_maximum_fusion = bf16[768,7168]{1,0:T(8,128)(2,1)} fusion(bf16[768,10]{1,0:T(8,128)(2,1)S(1)} %concatenate.28, bf16[768,768]{1,0:T(8,128)(2,1)} %fusion.76, bf16[768,3072]{1,0:T(8,128)(2,1)} %reshape.348, bf16[768,3072]{1,0:T(8,128)(2,1)} %fusion.64), kind=kLoop, calls=%fused_computation.7 | loop fusion | flops 55050240 | bytes 21642240 | tf_op jit(solution)/shard_map/scatter_late/concatenate | solution.py:207
  305.7 4.4 convolution_convert_fusion
  310.1 2.6 copy.128
  312.8 3.9 reshape.356
  316.7 21.0 %multiply_reduce_fusion = (f32[2,12,512]{2,1,0:T(8,128)S(1)}, f32[2,12,512,512]{2,3,1,0:T(8,128)}) fusion(f32[2,12,512]{2,1,0:T(8,128)S(1)} %log_add_fusion, f32[2,12,512,512]{2,3,1,0:T(8,128)} %get-tuple-element.129, pred[2,512]{1,0:T(4,128)(4,1)S(1)} %copy-done.28, bf16[2,512,12,64]{1,0,3,2:T(2,128)(2,1)} %reshape.337, bf16[2,512,12,64]{1,0,3,2:T(2,128)(2,1)} %reshape.356), kind=kOutput, calls=%fused_computation.1 | convolution fusion | flops 836751360 | bytes 53576704 | tf_op jit(solution)/shard_map/sqhd,skhd->shqk/dot_general | solution.py:249
  337.7 23.9 %multiply_convert_fusion = bf16[2,12,512,512]{2,3,1,0:T(8,128)(2,1)} fusion(f32[2,12,512,512]{2,3,1,0:T(8,128)} %get-tuple-element.141, f32[2,12,512]{2,1,0:T(8,128)S(1)} %get-tuple-element.140, f32[2,12,512]{2,1,0:T(8,128)S(1)} %log_add_fusion, f32[2,12,512,512]{2,3,1,0:T(8,128)} %get-tuple-element.129, pred[2,512]{1,0:T(4,128)(4,1)S(1)} %copy-done.28), kind=kLoop, calls=%fused_computation | loop fusion | flops 37748736 | bytes 63013888 | tf_op jit(solution)/shard_map/convert_element_type | solution.py:257
  361.7 8.5 %fusion.29 = bf16[2,512,12,64]{1,3,2,0:T(8,128)(2,1)S(1)} fusion(bf16[2,12,512,512]{2,3,1,0:T(8,128)(2,1)} %multiply_convert_fusion, bf16[2,512,12,64]{1,0,3,2:T(2,128)(2,1)S(1)} %copy-done.6), kind=kOutput, calls=%fused_computation.73 | convolution fusion | flops 806879232 | bytes 15728640 | tf_op jit(solution)/shard_map/shqk,sqhd->skhd/dot_general | solution.py:262
  370.2 1.6 copy.136
  371.8 1.6 copy.154
  373.4 6.9 %convert_reduce_fusion.2 = (bf16[12,64]{1,0:T(8,128)(2,1)S(1)}, bf16[2,512,12,64]{1,3,2,0:T(8,128)(2,1)S(1)}) fusion(bf16[2,12,512,512]{2,3,1,0:T(8,128)(2,1)} %multiply_convert_fusion, bf16[2,512,12,64]{1,0,3,2:T(2,128)(2,1)S(1)} %copy-done.4), kind=kOutput, calls=%fused_computation.43 | convolution fusion | flops 808451328 | bytes 15730176 | tf_op jit(solution)/shard_map/shqk,skhd->sqhd/dot_general | solution.py:258
  380.3 1.6 copy.133
  382.0 1.7 copy.153
  383.6 12.3 %convert_reduce_fusion.1 = (bf16[12,64]{1,0:T(8,128)(2,1)S(1)}, bf16[2,512,12,64]{1,3,2,0:T(8,128)(2,1)S(1)}) fusion(f32[2,12,512]{2,1,0:T(8,128)S(1)} %log_add_fusion, f32[2,12,512,512]{2,3,1,0:T(8,128)} %get-tuple-element.129, pred[2,512]{1,0:T(4,128)(4,1)S(1)} %copy-done.28, bf16[2,512,12,64]{1,0,3,2:T(2,128)(2,1)S(1)} %copy-done.12), kind=kOutput, calls=%fused_computation.42 | convolution fusion | flops 832830720 | bytes 28363264 | tf_op jit(solution)/shard_map/shqk,sqhd->skhd/dot_general | solution.py:252
  395.9 1.6 copy.139
  397.5 1.7 copy.155
  399.4 3.4 convolution_bitcast_fusion
  402.9 1.4 convolution_bitcast_fusion.1
  404.3 1.4 convolution_bitcast_fusion.2
  405.7 2.2 pad_maximum_fusion
  407.9 39.6 %reduce-scatter.5.cloned.1.call-done = bf16[24,7168]{1,0:T(8,128)(2,1)} async-done(((bf16[768,7168]{1,0:T(8,128)(2,1)}), bf16[24,7168]{1,0:T(8,128)(2,1)}) %reduce-scatter.5.cloned.1.call-update) | async-done | bytes 344080 | tf_op jit(solution)/shard_map/scatter_late/reduce_scatter | solution.py:71
  447.5 1.9 convert_element_type.260
  449.4 6.2 %copy.148 = bf16[768,2560]{1,0:T(8,128)(2,1)} copy(bf16[768,2560]{0,1:T(8,128)(2,1)} %pad_maximum_fusion) | data formatting | bytes 7864320
  455.6 3.3 fusion.46
  459.0 2.9 fusion.49
  461.9 4.6 add_convert_fusion.1
  469.3 1.7 slice_reduce_fusion
  471.0 88.5 %reduce-scatter.7.cloned.1.call-done = bf16[24,2560]{1,0:T(8,128)(2,1)} async-done(((bf16[768,2560]{1,0:T(8,128)(2,1)}), bf16[24,2560]{1,0:T(8,128)(2,1)}) %reduce-scatter.7.cloned.1.call-update) | async-done | bytes 122896
  559.5 1.2 copy.149
  (128 shorter events, 22.6 us)
Async XLA Ops:
  7.2 9.2 %copy-start = (bf16[2,128,768]{2,1,0:T(8,128)(2,1)S(1)}, bf16[2,128,768]{2,1,0:T(8,128)(2,1)}, u32[]{:S(2)}) copy-start(bf16[2,128,768]{2,1,0:T(8,128)(2,1)} %param.22) | copy-start | bytes 1179652
  7.2 12.9 %copy-start.32 = (s32[2]{0:T(128)S(1)}, s32[2]{0:T(128)}, u32[]{:S(2)}) copy-start(s32[2]{0:T(128)} %param.20) | copy-start | bytes 28
  7.2 72.4 %all-gather.3.cloned.1.call-start = ((), (), s32[]{:S(2)}) async-start(), calls=%async_computation.2 | async-start | bytes 5271552 | tf_op jit(solution)/shard_map/gather_attn/all_gather | solution.py:67
  11.2 0.7 copy-start.26
  11.9 152.9 %all-gather.5.cloned.1.call-start = ((), (), s32[]{:S(2)}) async-start(), calls=%async_computation.3 | async-start | bytes 10137600 | tf_op jit(solution)/shard_map/gather_ffn/all_gather | solution.py:67
  16.3 431.2 %reduce-scatter.5.cloned.1.call-start = ((), (), s32[]{:S(2)}) async-start(), calls=%async_computation.4 | async-start | bytes 11354112 | tf_op jit(solution)/shard_map/scatter_late/reduce_scatter | solution.py:71
  20.2 105.1 %copy-start.27 = (pred[2,512]{1,0:T(4,128)(4,1)}, pred[2,512]{1,0:T(4,128)(4,1)S(1)}, u32[]{:S(2)}) copy-start(pred[2,512]{1,0:T(4,128)(4,1)S(1)} %iota_compare_fusion.5) | copy-start | bytes 3076
  84.3 18.7 %copy-start.3 = (bf16[2,512,12,64]{1,0,3,2:T(2,128)(2,1)}, bf16[2,512,12,64]{1,0,3,2:T(2,128)(2,1)S(1)}, u32[]{:S(2)}) copy-start(bf16[2,512,12,64]{1,0,3,2:T(2,128)(2,1)S(1)} %reshape.339) | copy-start | bytes 4718596
  94.1 8.9 %copy-start.5 = (bf16[2,512,12,64]{1,0,3,2:T(2,128)(2,1)}, bf16[2,512,12,64]{1,0,3,2:T(2,128)(2,1)S(1)}, u32[]{:S(2)}) copy-start(bf16[2,512,12,64]{1,0,3,2:T(2,128)(2,1)S(1)} %reshape.338) | copy-start | bytes 4718596
  114.1 11.2 %copy-start.22 = (f32[2,12,512]{2,1,0:T(8,128)}, f32[2,12,512]{2,1,0:T(8,128)S(1)}, u32[]{:S(2)}) copy-start(f32[2,12,512]{2,1,0:T(8,128)S(1)} %get-tuple-element.128) | copy-start | bytes 147460
  114.1 11.2 %copy-start.11 = (bf16[2,512,12,64]{1,0,3,2:T(2,128)(2,1)S(1)}, bf16[2,512,12,64]{1,0,3,2:T(2,128)(2,1)}, u32[]{:S(2)}) copy-start(bf16[2,512,12,64]{1,0,3,2:T(2,128)(2,1)} %reshape.337) | copy-start | bytes 4718596
  125.4 13.2 %copy-start.24 = (f32[2,12,512]{2,1,0:T(8,128)}, f32[2,12,512]{2,1,0:T(8,128)S(1)}, u32[]{:S(2)}) copy-start(f32[2,12,512]{2,1,0:T(8,128)S(1)} %fusion) | copy-start | bytes 147460
  138.5 2.1 copy-start.33
  140.6 3.5 copy-start.16
  144.1 124.1 %copy-start.7 = (f32[1024,768]{1,0:T(8,128)}, f32[1024,768]{1,0:T(8,128)S(1)}, u32[]{:S(2)}) copy-start(f32[1024,768]{1,0:T(8,128)S(1)} %get-tuple-element.131) | copy-start | bytes 9437188
  144.6 1.0 copy-start.29
  171.5 10.1 %copy-start.31 = (f32[3072]{0:T(1024)S(1)}, f32[3072]{0:T(1024)}, u32[]{:S(2)}) copy-start(f32[3072]{0:T(1024)} %reshape.378) | copy-start | bytes 36868
  181.6 36.6 %copy-start.13 = (bf16[3072,768]{1,0:T(8,128)(2,1)S(1)}, bf16[3072,768]{1,0:T(8,128)(2,1)}, u32[]{:S(2)}) copy-start(bf16[3072,768]{1,0:T(8,128)(2,1)} %reshape.345) | copy-start | bytes 14155780
  223.6 1.9 copy-start.2
  229.2 1.7 copy-start.8
  256.6 11.7 %slice-start = ((s8[6291456]{0:T(1024)(128)(4,1)}), s8[4194304]{0:T(1024)(128)(4,1)S(1)}, s32[]{:S(2)}) async-start(s8[6291456]{0:T(1024)(128)(4,1)} %bitcast.130), calls=%async_computation.6 | async-start | bytes 8388608
  258.2 10.0 %copy-start.9 = (f32[1024,768]{1,0:T(8,128)S(1)}, f32[1024,768]{1,0:T(8,128)}, u32[]{:S(2)}) copy-start(f32[1024,768]{1,0:T(8,128)} %copy-done.8) | copy-start | bytes 9437188
  258.2 10.0 %slice-start.1 = ((s8[6291456]{0:T(1024)(128)(4,1)}), s8[2097152]{0:T(1024)(128)(4,1)S(1)}, s32[]{:S(2)}) async-start(s8[6291456]{0:T(1024)(128)(4,1)} %bitcast.130), calls=%async_computation.7 | async-start | bytes 4194304
  268.3 8.4 %copy-start.30 = (f32[1024]{0:T(1024)S(1)}, f32[1024]{0:T(1024)}, u32[]{:S(2)}) copy-start(f32[1024]{0:T(1024)} %copy-done.29) | copy-start | bytes 12292
  279.8 2.9 copy-start.17
  280.1 2.6 copy-start.15
  285.1 8.5 %copy-start.21 = (bf16[768,1]{1,0:T(8,128)(2,1)S(1)}, bf16[768,1]{1,0:T(8,128)(2,1)}, u32[]{:S(2)}) copy-start(bf16[768,1]{1,0:T(8,128)(2,1)} %reshape.384) | copy-start | bytes 4612
  304.8 0.8 copy-start.23
  304.8 0.9 copy-start.25
  304.8 254.7 %reduce-scatter.7.cloned.1.call-start = ((), (), s32[]{:S(2)}) async-start(), calls=%async_computation.5 | async-start | bytes 4055040
  310.1 6.6 %copy-start.28 = (pred[2,512]{1,0:T(4,128)(4,1)S(1)}, pred[2,512]{1,0:T(4,128)(4,1)}, u32[]{:S(2)}) copy-start(pred[2,512]{1,0:T(4,128)(4,1)} %copy-done.27) | copy-start | bytes 3076
  337.7 24.0 %copy-start.6 = (bf16[2,512,12,64]{1,0,3,2:T(2,128)(2,1)S(1)}, bf16[2,512,12,64]{1,0,3,2:T(2,128)(2,1)}, u32[]{:S(2)}) copy-start(bf16[2,512,12,64]{1,0,3,2:T(2,128)(2,1)} %copy-done.5) | copy-start | bytes 4718596
  370.2 3.2 copy-start.4
  380.3 3.3 copy-start.12
  399.4 3.4 copy-start.18
  399.4 3.4 copy-start.34
  402.9 1.4 copy-start.19
  455.6 3.3 copy-start.20
  459.0 2.9 copy-start.10
  461.9 4.6 copy-start.14
  469.3 94.5 %copy-start.1 = (bf16[2,128,768]{2,1,0:T(8,128)(2,1)S(1)}, bf16[2,128,768]{2,1,0:T(8,128)(2,1)}, u32[]{:S(2)}) copy-start(bf16[2,128,768]{2,1,0:T(8,128)(2,1)} %param.22) | copy-start | bytes 1179652
Sparse Core Ops, SparseCore 0:
  12.0 67.5 all-gather.2
  83.1 81.6 all-gather.4
  305.0 142.5 reduce-scatter.4
  455.7 103.7 reduce-scatter.6

commit v4 on v3

--- a/solution.py
+++ b/solution.py
@@ -71,6 +71,29 @@
     return lax.psum_scatter(pack.astype(GRAD_WIRE), AXES, scatter_dimension=0, tiled=True).astype(
         jnp.float32
     )
+
+
+def tree_scatter(full):
+    n_sub = lax.axis_size("sub")
+    n_f = lax.axis_size("fsdp")
+    rows = full.shape[0] // (n_sub * n_f)
+    acc = full.reshape(n_f, n_sub, rows, -1)
+    core = lax.axis_index("sub")
+    keep = lax.dynamic_index_in_dim(acc, core, 1, keepdims=False)
+    send = lax.dynamic_index_in_dim(acc, 1 - core, 1, keepdims=False)
+    acc = keep + lax.ppermute(send, "sub", [(0, 1), (1, 0)])
+    chip = lax.axis_index("fsdp")
+    bits = n_f.bit_length() - 1
+    acc = acc.reshape((2,) * bits + (rows, -1))
+    for j in range(bits):
+        axis = bits - 1 - j
+        bit = (chip >> j) & 1
+        keep = lax.dynamic_index_in_dim(acc, bit, axis, keepdims=False)
+        send = lax.dynamic_index_in_dim(acc, 1 - bit, axis, keepdims=False)
+        pairs = [(g, g ^ (1 << j)) for g in range(n_f)]
+        recv = lax.ppermute(send.astype(GRAD_WIRE), "fsdp", pairs)
+        acc = keep + recv.astype(jnp.float32)
+    return acc.reshape(rows, -1)
 
 
 def body(
@@ -284,8 +307,7 @@
             ],
             axis=1,
         )
-        qkv_pack, late_own = lax.optimization_barrier((qkv_pack, late_own))
-        qkv_own = scatter_rows(qkv_pack)
+        qkv_own = tree_scatter(qkv_pack)
     grad_query_own = qkv_own[:, 0:width]
     grad_key_own = qkv_own[:, width : 2 * width]
     grad_value_own = qkv_own[:, 2 * width : 3 * width]

time: 575 us -> 549 us (0.955)
  waiting for transfers between devices: 207 us -> 157 us
  local copies, waits for them, and re-layouts: 83.7 us -> 93.3 us
  other arithmetic: 64.8 us -> 72.6 us
  starting transfers between devices: 0.16 us -> 6.43 us
    unnamed x5 -> x3, waiting for transfers between devices: 88.6 us -> 0.05 us
    ppermute x0 -> x5, waiting for transfers between devices: none -> 63 us  [the longest x4 56.1 us: tree_scatter(): recv = lax.ppermute(send.astype(GRAD_WIRE), 'fsdp', pairs)]
    reduce_scatter x1, waiting for transfers between devices: 39.6 us -> 14.7 us  [scatter_rows(): lax.psum_scatter(pack.astype(GRAD_WIRE), AXES, scatter_dimension=0, tiled...]
    concatenate x0 -> x1, local copies, waits for them, and re-layouts: none -> 9.44 us  [body(): jnp.concatenate([grad_query, grad_key, grad_value, pack_vectors(width, (g...]
    unnamed x89 -> x82, local copies, waits for them, and re-layouts: 24 us -> 15.5 us
    add x0 -> x5, other arithmetic: none -> 8.16 us  [the longest x1 4.75 us: tree_scatter(): acc = keep + lax.ppermute(send, 'sub', [(0, 1), (1, 0)])]
    ppermute x0 -> x5, starting transfers between devices: none -> 6.31 us  [the longest x4 6.05 us: tree_scatter(): recv = lax.ppermute(send.astype(GRAD_WIRE), 'fsdp', pairs)]
  transfers between devices with their start and end apart: 4 -> 8, of which waited for: 4 -> 8; matrix products, arithmetic and copies ran while one was open for 33% -> 25% of each run, Pallas kernels for 0% -> 0%
where the time goes in v4:
time: 549 us; the launch traced here: 545 us
  matrix products  201 us (37%)
  waiting for transfers between devices  157 us (29%)
  local copies, waits for them, and re-layouts  93.3 us (17%)
  other arithmetic  72.6 us (13%)
  between operations  14.6 us (3%)
  starting transfers between devices  6.43 us (1%)
    all_gather x2, waiting for transfers between devices, gather_rows(): return lax.all_gather(pack, AXES, axis=0, tiled=True)  78.8 us
    dot_general x6, matrix products, project(): return jnp.dot(rows_low, weight, preferred_element_type=jnp.float32)  58.5 us
    ppermute x4, waiting for transfers between devices, tree_scatter(): recv = lax.ppermute(send.astype(GRAD_WIRE), 'fsdp', pairs)  56.1 us
    dot_general x6, matrix products, reverse_projection(): lax.dot_general(grad_low, weight, (((1,), (1,)), ((), ())), preferred_ele...  40.5 us
    dot_general x6, matrix products, weight_grad(): lax.dot_general(rows_low, grad_low, (((0,), (0,)), ((), ())), preferred_e...  26.1 us
    convert_element_type x1, other arithmetic, body(): scores_grad = (probs * (probs_grad - inner_sum)).astype(jnp.bfloat16)  21.7 us
    dot_general x1, matrix products, body(): jnp.einsum('sqhd,skhd->shqk', attended_grad, value_heads, preferred_eleme...  19.7 us
    unnamed x82, local copies, waits for them, and re-layouts  15.5 us
  transfers between devices with their start and end apart: 8, of which 8 were waited for; matrix products, arithmetic and copies ran while one was open for 25% of the time, Pallas kernels for 0%

profile of v4, /device:TPU:0, one launch (start us, length us, event | category | flops | bytes accessed | tf_op | source)
XLA Modules:
  0.0 544.9 jit_solution(15796244089579099442)
XLA Ops:
  14.7 1.7 fusion.58
  16.4 2.9 fusion.78
  20.2 59.4 %all-gather.3.cloned.1.call-done = bf16[768,3328]{1,0:T(8,128)(2,1)} async-done(((bf16[24,3328]{1,0:T(8,128)(2,1)}), bf16[768,3328]{1,0:T(8,128)(2,1)}) %all-gather.3.cloned.1.call-update) | async-done | bytes 5111824 | tf_op jit(solution)/shard_map/gather_attn/all_gather | solution.py:67
  79.6 3.2 fusion.30
  84.2 2.5 convert_reduce_fusion.9
  86.7 4.4 fusion.32
  91.2 2.9 reshape.348
  94.0 5.0 fusion.31
  99.0 3.9 reshape.347
  102.9 11.1 %fusion.12 = (f32[2,12,512]{2,1,0:T(8,128)S(1)}, f32[2,12,512,512]{2,3,1,0:T(8,128)}) fusion(pred[2,512]{1,0:T(4,128)(4,1)S(1)} %iota_compare_fusion.5, bf16[2,512,12,64]{1,0,3,2:T(2,128)(2,1)S(1)} %reshape.349, bf16[2,512,12,64]{1,0,3,2:T(2,128)(2,1)S(1)} %reshape.348), kind=kOutput, calls=%fused_computation.31 | convolution fusion | flops 824168448 | bytes 28361728 | tf_op jit(solution)/shard_map/sqhd,skhd->shqk/dot_general | solution.py:46
  114.0 11.2 %fusion = f32[2,12,512]{2,1,0:T(8,128)S(1)} fusion(f32[2,12,512]{2,1,0:T(8,128)S(1)} %get-tuple-element.58, f32[2,12,512,512]{2,3,1,0:T(8,128)} %get-tuple-element.59, pred[2,512]{1,0:T(4,128)(4,1)S(1)} %iota_compare_fusion.5), kind=kLoop, calls=%fused_computation.6 | loop fusion | flops 25153536 | bytes 25265152 | tf_op jit(solution)/shard_map/reduce_sum | solution.py:186
  125.3 12.8 %fusion.33 = bf16[2,512,12,64]{1,3,2,0:T(8,128)(2,1)S(1)} fusion(f32[2,12,512]{2,1,0:T(8,128)S(1)} %fusion, f32[2,12,512]{2,1,0:T(8,128)S(1)} %get-tuple-element.58, f32[2,12,512,512]{2,3,1,0:T(8,128)} %get-tuple-element.59, pred[2,512]{1,0:T(4,128)(4,1)S(1)} %iota_compare_fusion.5, bf16[2,512,12,64]{1,0,3,2:T(2,128)(2,1)S(1)} %copy-done.11), kind=kOutput, calls=%fused_computation.81 | convolution fusion | flops 837550080 | bytes 28410880 | tf_op jit(solution)/shard_map/shqk,skhd->sqhd/dot_general | solution.py:189
  138.1 1.6 copy.111
  140.2 3.5 fusion.76
  145.4 19.4 %all-gather.5.cloned.1.call-done = bf16[768,6400]{1,0:T(8,128)(2,1)} async-done(((bf16[24,6400]{1,0:T(8,128)(2,1)}), bf16[768,6400]{1,0:T(8,128)(2,1)}) %all-gather.5.cloned.1.call-update) | async-done | bytes 9830416 | tf_op jit(solution)/shard_map/gather_ffn/all_gather | solution.py:67
  166.6 4.9 slice.153
  171.5 8.5 %reshape.355 = bf16[3072,768]{1,0:T(8,128)(2,1)} reshape(bf16[768,3072]{1,0:T(8,128)(2,1)} %slice.153) | data formatting | bytes 9437184 | tf_op jit(solution)/shard_map/reshape | solution.py:166
  180.0 1.6 convert_reduce_fusion.6
  181.6 36.9 %multiply_convert_fusion.1 = (bf16[1024,3072]{1,0:T(8,128)(2,1)S(1)}, f32[1024,3072]{1,0:T(8,128)}, f32[1024,3072]{1,0:T(8,128)}) fusion(f32[3072]{0:T(1024)S(1)} %copy-done.30, bf16[768,6400]{1,0:T(8,128)(2,1)} %all-gather.5.cloned.1.call-done, f32[1024,768]{1,0:T(8,128)S(1)} %get-tuple-element.61, f32[768]{0:T(1024)S(1)} %get-tuple-element.29, ...), kind=kOutput, calls=%fused_computation.16 | convolution fusion | flops 5043388416 | bytes 39348224 | tf_op jit(solution)/shard_map/dot_general | solution.py:25
  218.5 5.4 fusion.77
  226.9 2.7 fusion.72
  229.6 1.7 copy-done.7
  231.7 7.0 %fusion.79 = bf16[3072,768]{1,0:T(8,128)(2,1)} fusion(bf16[1024,3072]{1,0:T(8,128)(2,1)S(1)} %get-tuple-element.50, bf16[1024,768]{1,0:T(8,128)(2,1)S(1)} %get-tuple-element.47), kind=kOutput, calls=%fused_computation.167 | convolution fusion | flops 4831838208 | bytes 12582912 | tf_op jit(solution)/shard_map/dot_general | solution.py:35
  238.7 17.0 %convert_reduce_fusion = (bf16[3072]{0:T(1024)(128)(2,1)S(1)}, bf16[1024,3072]{1,0:T(8,128)(2,1)}) fusion(f32[1024,3072]{1,0:T(8,128)} %get-tuple-element.51, bf16[1024,768]{1,0:T(8,128)(2,1)S(1)} %get-tuple-element.47, bf16[3072,768]{1,0:T(8,128)(2,1)} %reshape.355, f32[1024,3072]{1,0:T(8,128)} %get-tuple-element.62, f32[3072]{0:T(1024)S(1)} %copy-done.30), kind=kOutput, calls=%fused_computation.13 | convolution fusion | flops 4885312512 | bytes 37767168 | tf_op jit(solution)/shard_map/dot_general | solution.py:29
  258.5 10.0 %fusion.68 = bf16[768,3072]{1,0:T(8,128)(2,1)} fusion(bf16[1024,3072]{1,0:T(8,128)(2,1)} %get-tuple-element.66, f32[1024,768]{1,0:T(8,128)S(1)} %get-tuple-element.61, f32[768]{0:T(1024)S(1)} %get-tuple-element.29, f32[768]{0:T(1024)S(1)} %get-tuple-element.28, f32[1024]{0:T(1024)S(1)} %fusion.62, f32[1024]{0:T(1024)S(1)} %broadcast_multiply_fusion.1), kind=kOutput, calls=%fused_computation.159 | convolution fusion | flops 4835770368 | bytes 14170112 | tf_op jit(solution)/shard_map/dot_general | solution.py:35
  268.6 8.4 %multiply_reduce_fusion.1 = (bf16[768]{0:T(1024)(128)(2,1)S(1)}, f32[1024]{0:T(1024)S(1)}, bf16[768]{0:T(1024)(128)(2,1)S(1)}, f32[1024,768]{1,0:T(8,128)S(1)}) fusion(f32[1024,768]{1,0:T(8,128)S(1)} %get-tuple-element.61, f32[1024]{0:T(1024)S(1)} %fusion.62, f32[1024]{0:T(1024)S(1)} %broadcast_multiply_fusion.1, f32[768]{0:T(1024)S(1)} %get-tuple-element.28, ...), kind=kOutput, calls=%fused_computation.49 | convolution fusion | flops 4839699456 | bytes 20469760 | tf_op jit(solution)/shard_map/dot_general | solution.py:29
  277.0 3.3 fusion.71
  283.2 2.4 fusion.80
  285.7 8.5 %reshape.358 = bf16[768,3072]{1,0:T(8,128)(2,1)} reshape(bf16[3072,768]{1,0:T(8,128)(2,1)} %fusion.79) | data formatting | bytes 9437184 | tf_op jit(solution)/shard_map/scatter_late/reshape | solution.py:233
  294.2 1.7 concatenate.28
  295.9 9.5 %select_maximum_fusion = bf16[768,7168]{1,0:T(8,128)(2,1)} fusion(bf16[768,10]{1,0:T(8,128)(2,1)S(1)} %concatenate.28, bf16[768,768]{1,0:T(8,128)(2,1)} %fusion.80, bf16[768,3072]{1,0:T(8,128)(2,1)} %reshape.358, bf16[768,3072]{1,0:T(8,128)(2,1)} %fusion.68), kind=kLoop, calls=%fused_computation.7 | loop fusion | flops 55050240 | bytes 21642240 | tf_op jit(solution)/shard_map/scatter_late/concatenate | solution.py:230
  305.3 4.4 convolution_convert_fusion
  309.8 2.6 copy.121
  312.4 3.9 reshape.366
  316.3 19.7 %multiply_reduce_fusion = (f32[2,12,512]{2,1,0:T(8,128)S(1)}, f32[2,12,512,512]{2,3,1,0:T(8,128)}) fusion(f32[2,12,512]{2,1,0:T(8,128)S(1)} %copy-done.24, f32[2,12,512,512]{2,3,1,0:T(8,128)} %get-tuple-element.59, pred[2,512]{1,0:T(4,128)(4,1)S(1)} %copy-done.27, bf16[2,512,12,64]{1,0,3,2:T(2,128)(2,1)} %reshape.347, bf16[2,512,12,64]{1,0,3,2:T(2,128)(2,1)} %reshape.366), kind=kOutput, calls=%fused_computation.1 | convolution fusion | flops 836751360 | bytes 53576704 | tf_op jit(solution)/shard_map/sqhd,skhd->shqk/dot_general | solution.py:272
  336.0 12.5 %convert_reduce_fusion.1 = (f32[12,64]{1,0:T(8,128)S(1)}, bf16[2,512,12,64]{1,3,2,0:T(8,128)(2,1)}) fusion(f32[2,12,512]{2,1,0:T(8,128)S(1)} %copy-done.24, f32[2,12,512,512]{2,3,1,0:T(8,128)} %get-tuple-element.59, pred[2,512]{1,0:T(4,128)(4,1)S(1)} %copy-done.27, bf16[2,512,12,64]{1,0,3,2:T(2,128)(2,1)} %reshape.366), kind=kOutput, calls=%fused_computation.44 | convolution fusion | flops 832830720 | bytes 28364800 | tf_op jit(solution)/shard_map/shqk,sqhd->skhd/dot_general | solution.py:275
  348.5 21.7 %multiply_convert_fusion = bf16[2,12,512,512]{2,3,1,0:T(8,128)(2,1)} fusion(f32[2,12,512,512]{2,3,1,0:T(8,128)} %get-tuple-element.71, f32[2,12,512]{2,1,0:T(8,128)S(1)} %get-tuple-element.70, f32[2,12,512]{2,1,0:T(8,128)S(1)} %copy-done.24, f32[2,12,512,512]{2,3,1,0:T(8,128)} %get-tuple-element.59, pred[2,512]{1,0:T(4,128)(4,1)S(1)} %copy-done.27), kind=kLoop, calls=%fused_computation | loop fusion | flops 37748736 | bytes 63013888 | tf_op jit(solution)/shard_map/convert_element_type | solution.py:280
  370.3 9.6 %fusion.29 = bf16[2,512,12,64]{1,3,2,0:T(8,128)(2,1)} fusion(bf16[2,12,512,512]{2,3,1,0:T(8,128)(2,1)} %multiply_convert_fusion, bf16[2,512,12,64]{1,0,3,2:T(2,128)(2,1)S(1)} %copy-done.5), kind=kOutput, calls=%fused_computation.77 | convolution fusion | flops 806879232 | bytes 15728640 | tf_op jit(solution)/shard_map/shqk,sqhd->skhd/dot_general | solution.py:285
  379.9 7.6 %convert_reduce_fusion.2 = (f32[12,64]{1,0:T(8,128)S(1)}, bf16[2,512,12,64]{1,3,2,0:T(8,128)(2,1)S(1)}) fusion(bf16[2,12,512,512]{2,3,1,0:T(8,128)(2,1)} %multiply_convert_fusion, bf16[2,512,12,64]{1,0,3,2:T(2,128)(2,1)} %copy-done.3), kind=kOutput, calls=%fused_computation.45 | convolution fusion | flops 808451328 | bytes 15731712 | tf_op jit(solution)/shard_map/shqk,skhd->sqhd/dot_general | solution.py:281
  387.6 1.6 copy.129
  389.2 1.6 copy.143
  390.8 1.6 copy.126
  392.4 1.6 copy.142
  394.0 1.6 copy.132
  395.6 1.6 copy.144
  397.5 3.6 convolution_bitcast_fusion
  401.1 1.6 convolution_bitcast_fusion.1
  404.1 3.6 pad_maximum_fusion
  407.7 9.4 %copy.133 = f32[768,2560]{1,0:T(8,128)} copy(f32[768,2560]{0,1:T(8,128)} %pad_maximum_fusion) | data formatting | bytes 15728640 | tf_op jit(solution)/shard_map/scatter_qkv/concatenate | solution.py:301
  417.1 4.6 dynamic-slice_bitcast_fusion
  421.9 6.9 %collective-permute-done = f32[16,24,2560]{2,1,0:T(8,128)} collective-permute-done((f32[16,24,2560]{2,1,0:T(8,128)}, f32[16,24,2560]{2,1,0:T(8,128)}, u32[]{:S(2)}, u32[]{:S(2)}) %collective-permute-start) | collective-permute-done | bytes 3932192 | tf_op jit(solution)/shard_map/scatter_qkv/ppermute | solution.py:84
  428.8 4.8 bitcast_add_fusion
  433.6 1.9 copy-done.9
  437.4 31.6 %collective-permute-done.1 = bf16[2,2,2,24,2560]{4,3,2,1,0:T(8,128)(2,1)} collective-permute-done((bf16[2,2,2,24,2560]{4,3,2,1,0:T(8,128)(2,1)}, bf16[2,2,2,24,2560]{4,3,2,1,0:T(8,128)(2,1)}, u32[]{:S(2)}, u32[]{:S(2)}) %collective-permute-start.1) | collective-permute-done | bytes 983072 | tf_op jit(solution)/shard_map/scatter_qkv/ppermute | solution.py:94
  469.1 2.0 bitcast_add_fusion.1
  474.5 3.4 fusion.46
  477.9 8.2 %collective-permute-done.2 = bf16[2,2,24,2560]{3,2,1,0:T(8,128)(2,1)} collective-permute-done((bf16[2,2,24,2560]{3,2,1,0:T(8,128)(2,1)}, bf16[2,2,24,2560]{3,2,1,0:T(8,128)(2,1)}, u32[]{:S(2)}, u32[]{:S(2)}) %collective-permute-start.2) | collective-permute-done | bytes 491552 | tf_op jit(solution)/shard_map/scatter_qkv/ppermute | solution.py:94
  487.5 2.7 collective-permute-start.3
  490.2 2.7 fusion.49
  493.0 12.0 %collective-permute-done.3 = bf16[2,24,2560]{2,1,0:T(8,128)(2,1)S(1)} collective-permute-done((bf16[2,24,2560]{2,1,0:T(8,128)(2,1)S(1)}, bf16[2,24,2560]{2,1,0:T(8,128)(2,1)S(1)}, u32[]{:S(2)}, u32[]{:S(2)}) %collective-permute-start.3) | collective-permute-done | bytes 245792 | tf_op jit(solution)/shard_map/scatter_qkv/ppermute | solution.py:94
  506.2 4.6 add_convert_fusion.1
  510.8 4.2 collective-permute-done.4
  516.4 14.7 %reduce-scatter.2.cloned.1.call-done = bf16[24,7168]{1,0:T(8,128)(2,1)} async-done(((bf16[768,7168]{1,0:T(8,128)(2,1)}), bf16[24,7168]{1,0:T(8,128)(2,1)}) %reduce-scatter.2.cloned.1.call-update) | async-done | bytes 344080 | tf_op jit(solution)/shard_map/scatter_late/reduce_scatter | solution.py:71
  534.2 1.7 fusion.74
  (138 shorter events, 39.1 us)
Async XLA Ops:
  7.2 9.2 %copy-start = (bf16[2,128,768]{2,1,0:T(8,128)(2,1)S(1)}, bf16[2,128,768]{2,1,0:T(8,128)(2,1)}, u32[]{:S(2)}) copy-start(bf16[2,128,768]{2,1,0:T(8,128)(2,1)} %param.22) | copy-start | bytes 1179652
  7.2 13.0 %copy-start.31 = (s32[2]{0:T(128)S(1)}, s32[2]{0:T(128)}, u32[]{:S(2)}) copy-start(s32[2]{0:T(128)} %param.20) | copy-start | bytes 28
  7.2 72.4 %all-gather.3.cloned.1.call-start = ((), (), s32[]{:S(2)}) async-start(), calls=%async_computation.1 | async-start | bytes 5271552 | tf_op jit(solution)/shard_map/gather_attn/all_gather | solution.py:67
  11.2 0.7 copy-start.25
  11.9 152.9 %all-gather.5.cloned.1.call-start = ((), (), s32[]{:S(2)}) async-start(), calls=%async_computation.2 | async-start | bytes 10137600 | tf_op jit(solution)/shard_map/gather_ffn/all_gather | solution.py:67
  16.3 514.8 %reduce-scatter.2.cloned.1.call-start = ((), (), s32[]{:S(2)}) async-start(), calls=%async_computation.3 | async-start | bytes 11354112 | tf_op jit(solution)/shard_map/scatter_late/reduce_scatter | solution.py:71
  20.2 105.0 %copy-start.26 = (pred[2,512]{1,0:T(4,128)(4,1)}, pred[2,512]{1,0:T(4,128)(4,1)S(1)}, u32[]{:S(2)}) copy-start(pred[2,512]{1,0:T(4,128)(4,1)S(1)} %iota_compare_fusion.5) | copy-start | bytes 3076
  84.2 18.7 %copy-start.3 = (bf16[2,512,12,64]{1,0,3,2:T(2,128)(2,1)}, bf16[2,512,12,64]{1,0,3,2:T(2,128)(2,1)S(1)}, u32[]{:S(2)}) copy-start(bf16[2,512,12,64]{1,0,3,2:T(2,128)(2,1)S(1)} %reshape.349) | copy-start | bytes 4718596
  94.0 8.9 %copy-start.4 = (bf16[2,512,12,64]{1,0,3,2:T(2,128)(2,1)}, bf16[2,512,12,64]{1,0,3,2:T(2,128)(2,1)S(1)}, u32[]{:S(2)}) copy-start(bf16[2,512,12,64]{1,0,3,2:T(2,128)(2,1)S(1)} %reshape.348) | copy-start | bytes 4718596
  114.0 11.2 %copy-start.11 = (bf16[2,512,12,64]{1,0,3,2:T(2,128)(2,1)S(1)}, bf16[2,512,12,64]{1,0,3,2:T(2,128)(2,1)}, u32[]{:S(2)}) copy-start(bf16[2,512,12,64]{1,0,3,2:T(2,128)(2,1)} %reshape.347) | copy-start | bytes 4718596
  138.1 2.1 copy-start.32
  140.2 3.5 copy-start.20
  143.7 124.8 %copy-start.6 = (f32[1024,768]{1,0:T(8,128)}, f32[1024,768]{1,0:T(8,128)S(1)}, u32[]{:S(2)}) copy-start(f32[1024,768]{1,0:T(8,128)S(1)} %get-tuple-element.61) | copy-start | bytes 9437188
  144.2 1.1 copy-start.28
  171.5 10.1 %copy-start.30 = (f32[3072]{0:T(1024)S(1)}, f32[3072]{0:T(1024)}, u32[]{:S(2)}) copy-start(f32[3072]{0:T(1024)} %reshape.390) | copy-start | bytes 36868
  181.6 36.9 %copy-start.15 = (bf16[3072,768]{1,0:T(8,128)(2,1)S(1)}, bf16[3072,768]{1,0:T(8,128)(2,1)}, u32[]{:S(2)}) copy-start(bf16[3072,768]{1,0:T(8,128)(2,1)} %reshape.355) | copy-start | bytes 14155780
  224.0 1.9 copy-start.2
  229.6 1.7 copy-start.7
  256.8 11.7 %slice-start = ((s8[6291456]{0:T(1024)(128)(4,1)}), s8[4194304]{0:T(1024)(128)(4,1)S(1)}, s32[]{:S(2)}) async-start(s8[6291456]{0:T(1024)(128)(4,1)} %bitcast.151), calls=%async_computation.4 | async-start | bytes 8388608
  258.5 10.0 %copy-start.8 = (f32[1024,768]{1,0:T(8,128)S(1)}, f32[1024,768]{1,0:T(8,128)}, u32[]{:S(2)}) copy-start(f32[1024,768]{1,0:T(8,128)} %copy-done.7) | copy-start | bytes 9437188
  258.5 10.0 %slice-start.1 = ((s8[6291456]{0:T(1024)(128)(4,1)}), s8[2097152]{0:T(1024)(128)(4,1)S(1)}, s32[]{:S(2)}) async-start(s8[6291456]{0:T(1024)(128)(4,1)} %bitcast.151), calls=%async_computation.5 | async-start | bytes 4194304
  268.6 8.4 %copy-start.29 = (f32[1024]{0:T(1024)S(1)}, f32[1024]{0:T(1024)}, u32[]{:S(2)}) copy-start(f32[1024]{0:T(1024)} %copy-done.28) | copy-start | bytes 12292
  280.3 2.9 copy-start.21
  280.7 2.6 copy-start.16
  285.7 8.5 %copy-start.23 = (bf16[768,1]{1,0:T(8,128)(2,1)S(1)}, bf16[768,1]{1,0:T(8,128)(2,1)}, u32[]{:S(2)}) copy-start(bf16[768,1]{1,0:T(8,128)(2,1)} %reshape.396) | copy-start | bytes 4612
  309.8 6.5 %copy-start.24 = (f32[2,12,512]{2,1,0:T(8,128)S(1)}, f32[2,12,512]{2,1,0:T(8,128)}, u32[]{:S(2)}) copy-start(f32[2,12,512]{2,1,0:T(8,128)} %log_add_fusion) | copy-start | bytes 147460
  309.8 6.5 %copy-start.27 = (pred[2,512]{1,0:T(4,128)(4,1)S(1)}, pred[2,512]{1,0:T(4,128)(4,1)}, u32[]{:S(2)}) copy-start(pred[2,512]{1,0:T(4,128)(4,1)} %copy-done.26) | copy-start | bytes 3076
  348.5 21.8 %copy-start.5 = (bf16[2,512,12,64]{1,0,3,2:T(2,128)(2,1)S(1)}, bf16[2,512,12,64]{1,0,3,2:T(2,128)(2,1)}, u32[]{:S(2)}) copy-start(bf16[2,512,12,64]{1,0,3,2:T(2,128)(2,1)} %copy-done.4) | copy-start | bytes 4718596
  379.9 7.6 %copy-start.12 = (bf16[2,512,12,64]{1,3,2,0:T(8,128)(2,1)S(1)}, bf16[2,512,12,64]{1,3,2,0:T(8,128)(2,1)}, u32[]{:S(2)}) copy-start(bf16[2,512,12,64]{1,3,2,0:T(8,128)(2,1)} %fusion.29) | copy-start | bytes 4718596
  390.8 3.2 copy-start.22
  397.4 3.6 copy-start.19
  397.4 3.6 copy-start.33
  401.1 1.6 copy-start.17
  421.7 7.1 %collective-permute-start = (f32[16,24,2560]{2,1,0:T(8,128)}, f32[16,24,2560]{2,1,0:T(8,128)}, u32[]{:S(2)}, u32[]{:S(2)}) collective-permute-start(f32[16,24,2560]{2,1,0:T(8,128)} %dynamic-slice_bitcast_fusion), channel_id=1, source_target_pairs={{0,1},{1,0},{2,3},{3,2},{4,5},{5,4},{6,7},{7,6},{8,9},{9,8},{10,11... | collective-permute-start | bytes 11796488 | tf_op jit(solution)/shard_map/scatter_qkv/ppermute | solution.py:84
  433.6 1.9 copy-start.9
  436.5 32.6 %collective-permute-start.1 = (bf16[2,2,2,24,2560]{4,3,2,1,0:T(8,128)(2,1)}, bf16[2,2,2,24,2560]{4,3,2,1,0:T(8,128)(2,1)}, u32[]{:S(2)}, u32[]{:S(2)}) collective-permute-start(bf16[2,2,2,24,2560]{4,3,2,1,0:T(8,128)(2,1)} %fusion.54), channel_id=1, source_target_pairs={{0,2},{2,0},{4,6},{6,4},{8,10},{10,8},{12,14},{14,12},{16,18},{18,... | collective-permute-start | bytes 2949128 | tf_op jit(solution)/shard_map/scatter_qkv/ppermute | solution.py:94
  471.1 1.3 copy-start.13
  473.2 12.9 %collective-permute-start.2 = (bf16[2,2,24,2560]{3,2,1,0:T(8,128)(2,1)}, bf16[2,2,24,2560]{3,2,1,0:T(8,128)(2,1)}, u32[]{:S(2)}, u32[]{:S(2)}) collective-permute-start(bf16[2,2,24,2560]{3,2,1,0:T(8,128)(2,1)} %fusion.57), channel_id=1, source_target_pairs={{0,4},{2,6},{4,0},{6,2},{8,12},{10,14},{12,8},{14,10},{16,20},{18,... | collective-permute-start | bytes 1474568 | tf_op jit(solution)/shard_map/scatter_qkv/ppermute | solution.py:94
  474.5 11.6 %copy-start.14 = (f32[2,2,2,24,2560]{4,3,2,1,0:T(8,128)S(1)}, f32[2,2,2,24,2560]{4,3,2,1,0:T(8,128)}, u32[]{:S(2)}) copy-start(f32[2,2,2,24,2560]{4,3,2,1,0:T(8,128)} %copy-done.13) | copy-start | bytes 5898244
  474.5 15.7 %copy-start.18 = (bf16[96,8,2,512]{3,1,2,0:T(8,128)(2,1)S(1)}, bf16[96,8,2,512]{3,1,2,0:T(8,128)(2,1)}, u32[]{:S(2)}) copy-start(bf16[96,8,2,512]{3,1,2,0:T(8,128)(2,1)} %copy.142) | copy-start | bytes 4718596
  487.5 18.7 %copy-start.10 = (bf16[96,8,2,512]{3,1,2,0:T(8,128)(2,1)S(1)}, bf16[96,8,2,512]{3,1,2,0:T(8,128)(2,1)}, u32[]{:S(2)}) copy-start(bf16[96,8,2,512]{3,1,2,0:T(8,128)(2,1)} %copy.144) | copy-start | bytes 4718596
  487.5 17.5 %collective-permute-start.3 = (bf16[2,24,2560]{2,1,0:T(8,128)(2,1)S(1)}, bf16[2,24,2560]{2,1,0:T(8,128)(2,1)S(1)}, u32[]{:S(2)}, u32[]{:S(2)}) collective-permute-start(bf16[2,24,2560]{2,1,0:T(8,128)(2,1)S(1)} %fusion.60), channel_id=1, source_target_pairs={{0,8},{2,10},{4,12},{6,14},{8,0},{10,2},{12,4},{14,6},{16,24},{18,... | collective-permute-start | bytes 737288 | tf_op jit(solution)/shard_map/scatter_qkv/ppermute | solution.py:94
  505.1 9.9 %collective-permute-start.4 = (bf16[24,2560]{1,0:T(8,128)(2,1)S(1)}, bf16[24,2560]{1,0:T(8,128)(2,1)S(1)}, u32[]{:S(2)}, u32[]{:S(2)}) collective-permute-start(bf16[24,2560]{1,0:T(8,128)(2,1)S(1)} %fusion.61), channel_id=1, source_target_pairs={{0,16},{2,18},{4,20},{6,22},{8,24},{10,26},{12,28},{14,30},{16,0},... | collective-permute-start | bytes 368648 | tf_op jit(solution)/shard_map/scatter_qkv/ppermute | solution.py:94
  506.2 31.9 %copy-start.1 = (bf16[2,128,768]{2,1,0:T(8,128)(2,1)S(1)}, bf16[2,128,768]{2,1,0:T(8,128)(2,1)}, u32[]{:S(2)}) copy-start(bf16[2,128,768]{2,1,0:T(8,128)(2,1)} %param.22) | copy-start | bytes 1179652
Sparse Core Ops, SparseCore 0:
  12.0 67.5 all-gather.2
  83.1 81.7 all-gather.4
  380.0 151.0 reduce-scatter.1
